TPU v7x, 32 devices: a whole 2x2x4 slice. The times are simulated.
32 devices in a mesh: zon: 8 (over z, y), mer: 4 (over x, core).
Axes of the slice: x: 2, y: 2, z: 4, core: 2. Of those that a mesh axis runs over, the one named last changes fastest.
Arguments:
- sea_level: float32 [512, 4096], P('mer', 'zon'), may hold values from -6 to 6
- forcing: float32 [512, 4096], P('mer', 'zon'), may hold values from -6 to 6
- link_weights: float32 [8, 512, 4096], P(None, 'mer', 'zon'), may hold values from 0.1 to 2
- excess: float32 [512, 4096], P('mer', 'zon'), may hold values from 0.05 to 0.5
- ocean_mask: int32 [512, 4096], P('mer', 'zon'), may hold values 0 or 1
- current: float32 [2, 512, 4096], P(None, 'mer', 'zon'), may hold values from -6 to 6
- intersection_block: int32 [32, 32, 32], P(('zon', 'mer')), may hold values from -1 to 511, as said below
- intersection_cols: int32 [32, 32, 32, 128], P(('zon', 'mer')), may hold values from -1 to 127, as said below
- ice_mass: float32 [32, 32, 32, 128], P(('zon', 'mer')), may hold values from 0.2 to 3
- coriolis: float32 [32, 32, 32, 128], P(('zon', 'mer')), may hold values from -1.5 to 1.5
- ice_start: float32 [2, 32, 32, 32, 128], P(None, ('zon', 'mer')), may hold values from -6 to 6
- wind_stress: float32 [2, 32, 32, 32, 128], P(None, ('zon', 'mer')), may hold values from -6 to 6
Outputs:
- surface: float32 [512, 4096], P('mer', 'zon')
- velocity: float32 [2, 32, 32, 32, 128], P(None, ('zon', 'mer'))
Inputs may be any that keep to these rules, and one draw needn't show every extreme that they name: `intersection_block`: for each owner device and ice device, the live ocean block numbers come first among the 32 slots and empty slots hold -1; in every draw one ice device receives 32 live blocks from every owner device. `intersection_cols`: within a live intersection block the cells named by different rows are distinct; rows of empty slots are all -1.
All inputs are finite; a program needn't handle non-finite values. No bound on the sum of `ocean_mask` on one device may be relied on, other than what follows from the above.
Results may differ from a plain program's by a relative error of at most 0.00002.
Values sent between devices are 32-bit elements; how exact they have to be, the bound alone decides.
A program may use at most 256 MiB of HBM per device.

v0:
```python
import jax
import jax.numpy as jnp
from jax import lax
from jax.sharding import PartitionSpec as P

SWEEPS = 2
ICE_SWEEPS = 3


drag_coeff = 1.0
link_coeff = 0.5
neighbour_steps = ((0, 1), (0, -1), (1, 0), (-1, 0), (1, 1), (1, -1), (-1, 1), (-1, -1))


def padded_2(shard, sides, width, wrap):
    for axis, dim in sides:
        count, length = (lax.axis_size(axis), shard.shape[dim])
        up = [(i, (i + 1) % count) for i in range(count if wrap else count - 1)]
        down = [(j, i) for i, j in up]
        last = lax.slice_in_dim(shard, length - width, length, axis=dim)
        first = lax.slice_in_dim(shard, 0, width, axis=dim)
        before = lax.ppermute(last, axis, up)
        after = lax.ppermute(first, axis, down)
        shard = jnp.concatenate([before, shard, after], axis=dim)
    return shard


def colour_sequence(sweep_count):
    return [0] + [1, 2, 3, 2, 1, 0] * sweep_count


def gauss_seidel(surface, source, link_weights, diagonal, is_ocean, pad_fn):
    row_count, col_count = surface.shape
    row_parity = lax.broadcasted_iota(jnp.int32, (row_count, col_count), 0) % 2
    col_parity = lax.broadcasted_iota(jnp.int32, (row_count, col_count), 1) % 2
    colours = 2 * row_parity + col_parity
    for colour in colour_sequence(SWEEPS):
        padded = pad_fn(surface)
        gathered = source
        for position, (row_step, col_step) in enumerate(neighbour_steps):
            gathered = (
                gathered
                + link_weights[position]
                * padded[
                    1 + row_step : 1 + row_step + row_count, 1 + col_step : 1 + col_step + col_count
                ]
            )
        surface = jnp.where(is_ocean & (colours == colour), gathered / diagonal, surface)
    return surface


def zero_pad(surface):
    return jnp.pad(surface, 1)


def along_block(values):
    padded = jnp.pad(values, [(0, 0)] * (values.ndim - 1) + [(1, 1)])
    return padded[..., :-2] + padded[..., 2:]


def ice_momentum(ice_mass, coriolis, ice_start, wind_stress, current):
    diagonal = ice_mass + drag_coeff + 2.0 * link_coeff
    turning = coriolis * ice_mass
    determinant = diagonal * diagonal + turning * turning
    base_east = ice_mass * ice_start[0] + wind_stress[0] + drag_coeff * current[0]
    base_north = ice_mass * ice_start[1] + wind_stress[1] + drag_coeff * current[1]
    velocity = ice_start
    for sweep_index in range(ICE_SWEEPS):
        beside = along_block(velocity)
        right_east = base_east + link_coeff * beside[0]
        right_north = base_north + link_coeff * beside[1]
        velocity = jnp.stack(
            [
                (diagonal * right_east + turning * right_north) / determinant,
                (diagonal * right_north - turning * right_east) / determinant,
            ]
        )
    return velocity


def to_ice(values):
    moved = lax.all_to_all(values, ("zon", "mer"), split_axis=2, concat_axis=1, tiled=True)
    return moved.reshape(values.shape)


def to_ocean(values):
    moved = lax.all_to_all(values, ("zon", "mer"), split_axis=2, concat_axis=1, tiled=True)
    return moved.reshape(values.shape)


def local(
    sea_level,
    forcing,
    link_weights,
    excess,
    ocean_mask,
    current,
    intersection_block,
    intersection_cols,
    ice_mass,
    coriolis,
    ice_start,
    wind_stress,
):
    row_count, col_count = sea_level.shape
    block = intersection_cols.shape[-1]
    cell_count = row_count * col_count
    slot_shape = intersection_block.shape[1:]
    slot_count = slot_shape[0] * slot_shape[1]
    slot_blocks = intersection_block[0].reshape(slot_count)
    slot_cols = intersection_cols[0].reshape(slot_count, block)
    is_valid = slot_cols >= 0
    target = jnp.where(
        is_valid, jnp.maximum(slot_blocks, 0)[:, None] * block + slot_cols, cell_count
    )
    flat_target = target.reshape(slot_count * block)
    flat_current = current.reshape(2, cell_count)
    fetched = jnp.take(flat_current, jnp.minimum(flat_target, cell_count - 1), axis=1)
    values = jnp.where(is_valid.reshape(1, slot_count * block), fetched, 0.0)
    values = values.reshape(2, slot_shape[0], slot_shape[1], block)
    ice_current = to_ice(values[:, None])
    velocity = ice_momentum(ice_mass, coriolis, ice_start, wind_stress, ice_current)
    ice_drag = drag_coeff * (velocity - ice_current)
    returned = to_ocean(ice_drag)[:, 0].reshape(2, slot_count * block)
    stress_grid = (
        jnp.zeros((2, cell_count), jnp.float32).at[:, flat_target].add(returned, mode="drop")
    )
    stress_grid = stress_grid.reshape(2, row_count, col_count)
    cycle_north = padded_2(stress_grid[1], (("zon", 1),), 1, True)
    lat_east = padded_2(stress_grid[0], (("mer", 0),), 1, False)
    zonal_diff = cycle_north[:, 2:] - cycle_north[:, :-2]
    meridional_diff = lat_east[2:] - lat_east[:-2]
    source = forcing + zonal_diff - meridional_diff
    is_ocean = ocean_mask > 0
    surface = jnp.where(is_ocean, sea_level, 0.0)
    rim_width = 6 * SWEEPS + 2
    stacked = jnp.concatenate(
        [
            surface[None],
            source[None],
            link_weights,
            excess[None],
            ocean_mask.astype(jnp.float32)[None],
        ],
        axis=0,
    )
    cycle_ext = padded_2(stacked, (("zon", 2),), rim_width, True)
    widened = padded_2(cycle_ext, (("mer", 1),), rim_width, False)
    wide_ocean = widened[11] > 0.5
    wide_diagonal = jnp.where(wide_ocean, (1.0 + widened[10]) * jnp.sum(widened[2:10], axis=0), 1.0)
    result = gauss_seidel(
        widened[0], widened[1], widened[2:10], wide_diagonal, wide_ocean, zero_pad
    )
    surface = result[rim_width : rim_width + row_count, rim_width : rim_width + col_count]
    return (surface, velocity)


def solution(mesh):
    return jax.shard_map(
        local,
        mesh=mesh,
        in_specs=(
            P("mer", "zon"),
            P("mer", "zon"),
            P(None, "mer", "zon"),
            P("mer", "zon"),
            P("mer", "zon"),
            P(None, "mer", "zon"),
            P(("zon", "mer"), None, None),
            P(("zon", "mer"), None, None, None),
            P(("zon", "mer"), None, None, None),
            P(("zon", "mer"), None, None, None),
            P(None, ("zon", "mer"), None, None, None),
            P(None, ("zon", "mer"), None, None, None),
        ),
        out_specs=(P("mer", "zon"), P(None, ("zon", "mer"), None, None, None)),
        check_vma=False,
    )
```

profile of v0, /device:TPU:1, one launch (start us, length us, event | category | flops | bytes accessed | tf_op | source)
XLA Modules:
  0.0 1452.1 jit_solution(13687160340592624859)
XLA Ops:
  1.7 3.1 compare_select_fusion
  4.9 16.5 %copy.58 = f32[2,128,512]{0,2,1:T(8,128)} copy(f32[2,128,512]{2,1,0:T(8,128)S(1)} %copy-done.4) | data formatting | bytes 1048576 | tf_op args[5]
  21.4 443.8 %gather_fusion = f32[131072,2]{1,0:T(8,128)} fusion(f32[2,65536]{0,1:T(8,128)} %bitcast.390, s32[131072]{0:T(1024)S(1)} %broadcast_clamp_fusion), kind=kCustom, calls=%fused_computation | custom fusion | bytes 2621440 | tf_op jit(solution)/shard_map/jit(_take)/gather | solution.py:118
  465.2 36.7 %copy.59 = f32[2,1,32,32,128]{4,3,1,0,2:T(8,128)S(1)} copy(f32[2,1,32,32,128]{0,4,3,2,1:T(8,128)} %bitcast.11) | data formatting | bytes 2097152 | tf_op jit(solution)/shard_map/jit(_take)/gather | solution.py:118
  503.5 7.1 all-to-all-start
  510.6 2.2 fusion.3
  512.8 23.0 %all-to-all-done = f32[2,1,32,32,128]{4,3,1,0,2:T(8,128)S(1)} async-done(((f32[2,1,32,32,128]{4,3,1,0,2:T(8,128)}), f32[2,1,32,32,128]{4,3,1,0,2:T(8,128)S(1)}, u32[]{:S(2)}, u32[]{:S(2)}) %all-to-all-start) | async-done | bytes 1048608 | tf_op jit(solution)/shard_map/all_to_all | solution.py:82
  535.8 2.3 divide_bitcast_fusion.5
  541.3 1.6 pad_maximum_fusion.2
  542.9 15.3 %all-to-all-start.1 = ((f32[2,1,32,32,128]{4,3,1,0,2:T(8,128)}), f32[2,1,32,32,128]{4,3,1,0,2:T(8,128)}, u32[]{:S(2)}, u32[]{:S(2)}) async-start(f32[2,1,32,32,128]{4,3,1,0,2:T(8,128)} %get-tuple-element.37), calls=%async_computation.1 | async-start | bytes 2097152 | tf_op jit(solution)/shard_map/all_to_all | solution.py:87
  561.6 21.7 %all-to-all-done.1 = f32[2,1,32,32,128]{4,3,1,0,2:T(8,128)} async-done(((f32[2,1,32,32,128]{4,3,1,0,2:T(8,128)}), f32[2,1,32,32,128]{4,3,1,0,2:T(8,128)}, u32[]{:S(2)}, u32[]{:S(2)}) %all-to-all-start.1) | async-done | bytes 1048608 | tf_op jit(solution)/shard_map/all_to_all | solution.py:87
  583.3 2.3 copy.63
  585.6 2.9 reshape.263
  588.5 30.1 %copy.64 = f32[131072,2]{1,0:T(8,128)} copy(f32[131072,2]{0,1:T(2,128)} %bitcast.391) | data formatting | bytes 2097152 | tf_op jit(solution)/shard_map/reshape;squeeze;reshape | solution.py:124
  618.6 706.8 %scatter_custom_fusion = f32[2,65536]{0,1:T(8,128)} fusion(s32[131072]{0:T(1024)} %bitcast.395, f32[131072,2]{1,0:T(8,128)} %copy.64, f32[]{:T(128)} %constant.24.clone.1), kind=kCustom, calls=%fused_computation.4 | custom fusion | flops 262144 | bytes 524800 | tf_op jit(solution)/shard_map/scatter-add | solution.py:126
  1325.4 34.7 %slice_reduce_fusion.1 = (f32[65536]{0:T(1024)}, f32[65536]{0:T(1024)}) fusion(f32[2,65536]{0,1:T(8,128)} %scatter_custom_fusion), kind=kLoop, calls=%fused_computation.3 | loop fusion | bytes 1048576 | tf_op jit(solution)/shard_map/slice | solution.py:129
  1360.2 1.9 fusion.196
  1362.0 1.7 squeeze.42
  1363.7 3.2 collective-permute-start.2
  1366.9 3.0 collective-permute-start.3
  1369.9 1.6 fusion.199
  1371.5 2.3 collective-permute-start
  1373.8 2.9 copy.70
  1376.7 1.8 copy.67
  1378.5 1.7 squeeze.43
  1382.3 2.2 fusion.181
  1384.5 1.8 copy.69
  1387.3 1.7 constant_dynamic-update-slice_fusion
  1390.5 2.9 collective-permute-start.5
  1393.4 2.6 collective-permute-done.4
  1396.4 3.8 fusion.197
  1400.2 3.3 copy.71
  1403.5 4.0 collective-permute-start.6
  1407.5 3.3 copy.72
  1410.9 2.0 collective-permute-start.7
  1412.9 2.3 copy.76
  1415.2 3.2 copy.73
  1418.4 2.9 collective-permute-done.7
  1421.3 3.2 copy.74
  1424.5 6.0 pad_maximum_fusion
  1431.0 1.6 divide_select_fusion.11
  1432.7 1.5 divide_select_fusion.10
  1434.2 1.5 divide_select_fusion.9
  1435.7 1.5 divide_select_fusion.8
  1442.9 1.5 divide_select_fusion.3
  1444.4 1.5 divide_select_fusion.2
  1446.0 1.5 divide_select_fusion.1
  1447.5 1.6 divide_select_fusion
  (59 shorter events, 22.7 us)
Async XLA Ops:
  0.6 4.2 copy-start.4
  465.2 36.7 %copy-start.1 = (s32[1,32,32,128]{3,2,1,0:T(8,128)S(1)}, s32[1,32,32,128]{3,2,1,0:T(8,128)}, u32[]{:S(2)}) copy-start(s32[1,32,32,128]{3,2,1,0:T(8,128)} %param.19) | copy-start | bytes 1572868
  502.3 33.5 %copy-start = (f32[1,32,32,128]{3,2,1,0:T(8,128)S(1)}, f32[1,32,32,128]{3,2,1,0:T(8,128)}, u32[]{:S(2)}) copy-start(f32[1,32,32,128]{3,2,1,0:T(8,128)} %param.20) | copy-start | bytes 1572868
  503.5 32.3 %all-to-all-start = ((f32[2,1,32,32,128]{4,3,1,0,2:T(8,128)}), f32[2,1,32,32,128]{4,3,1,0,2:T(8,128)S(1)}, u32[]{:S(2)}, u32[]{:S(2)}) async-start(f32[2,1,32,32,128]{4,3,1,0,2:T(8,128)} %select_select_fusion), calls=%async_computation | async-start | bytes 2097152 | tf_op jit(solution)/shard_map/all_to_all | solution.py:82
  541.3 17.0 %copy-start.2 = (s32[131072,1]{0,1:T(1,128)S(1)}, s32[131072,1]{0,1:T(1,128)}, u32[]{:S(2)}) copy-start(s32[131072,1]{0,1:T(1,128)} %get-tuple-element.19) | copy-start | bytes 1572868
  541.3 18.3 %copy-start.5 = (s32[128,512]{1,0:T(8,128)S(1)}, s32[128,512]{1,0:T(8,128)}, u32[]{:S(2)}) copy-start(s32[128,512]{1,0:T(8,128)} %param.16) | copy-start | bytes 786436
  541.3 18.5 %copy-start.6 = (f32[128,512]{1,0:T(8,128)S(1)}, f32[128,512]{1,0:T(8,128)}, u32[]{:S(2)}) copy-start(f32[128,512]{1,0:T(8,128)} %param.12) | copy-start | bytes 786436
  542.9 40.4 %all-to-all-start.1 = ((f32[2,1,32,32,128]{4,3,1,0,2:T(8,128)}), f32[2,1,32,32,128]{4,3,1,0,2:T(8,128)}, u32[]{:S(2)}, u32[]{:S(2)}) async-start(f32[2,1,32,32,128]{4,3,1,0,2:T(8,128)} %get-tuple-element.37), calls=%async_computation.1 | async-start | bytes 2097152 | tf_op jit(solution)/shard_map/all_to_all | solution.py:87
  1363.7 16.4 %collective-permute-start.2 = (f32[1,512]{0,1:T(8,128)}, f32[1,512]{0,1:T(8,128)}, u32[]{:S(2)}, u32[]{:S(2)}) collective-permute-start(f32[1,512]{0,1:T(8,128)} %get-tuple-element.20), channel_id=1, source_target_pairs={{1,0},{2,1},{3,2},{5,4},{6,5},{7,6},{9,8},{10,9},{11,10},{13,12},{... | collective-permute-start | bytes 6152 | tf_op jit(solution)/shard_map/ppermute | solution.py:23
  1366.9 14.3 collective-permute-start.3
  1371.5 10.8 collective-permute-start
  1373.8 8.5 collective-permute-start.1
  1386.3 2.8 copy-start.3
  1389.1 6.9 collective-permute-start.4
  1390.5 5.6 collective-permute-start.5
  1403.5 11.7 collective-permute-start.6
  1410.9 10.5 collective-permute-start.7
where the time goes:
time: 1460 us; the launch traced here: 1450 us
  other arithmetic  753 us (52%)
  local copies, waits for them, and re-layouts  607 us (42%)
  waiting for transfers between devices  50.3 us (3%)
  starting transfers between devices  41.2 us (3%)
    scatter-add x1, other arithmetic, local(): jnp.zeros((2, cell_count), jnp.float32).at[:, flat_target]  707 us
    gather x2, local copies, waits for them, and re-layouts, local(): jnp.take(flat_current, jnp.minimum(flat_target, cell_count - 1), axis=1)  481 us
    slice x1, local copies, waits for them, and re-layouts, local(): cycle_north = padded_2(stress_grid[1], (('zon', 1),), 1, True)  34.7 us
    another operation x2, local copies, waits for them, and re-layouts, local(): returned = to_ocean(ice_drag)[:, 0].reshape(2, slot_count * block)  33 us
  transfers between devices with their start and end apart: 10, of which 4 were waited for; matrix products, arithmetic and copies ran while one was open for 2% of the time, Pallas kernels for 0%

commit v1 on v0

v1 whole, which is shorter than its diff:
```python
import functools

import jax
import jax.numpy as jnp
from jax import lax
from jax.experimental import pallas as pl
from jax.experimental.pallas import tpu as pltpu
from jax.sharding import PartitionSpec as P

SWEEPS = 2
ICE_SWEEPS = 3
ROW_RIM = 8
COL_RIM = 16
LANES = 128

drag_coeff = 1.0
link_coeff = 0.5
VM = pl.BlockSpec(memory_space=pltpu.VMEM)
PARAMS = pltpu.CompilerParams(vmem_limit_bytes=48 * 1024 * 1024)


def cost(flops, nbytes):
    return pl.CostEstimate(flops=flops, bytes_accessed=nbytes, transcendentals=0)


def lane_take(values, index):
    return jnp.take_along_axis(values, index, axis=1, mode="promise_in_bounds")


def split3(values):
    high = values.astype(jnp.bfloat16)
    rest = values - high.astype(jnp.float32)
    middle = rest.astype(jnp.bfloat16)
    low = (rest - middle.astype(jnp.float32)).astype(jnp.bfloat16)
    return high, middle, low


def nn_dot(a, b):
    return lax.dot_general(a, b, (((1,), (0,)), ((), ())), preferred_element_type=jnp.float32)


def block_rows(blocks, tiles, rows):
    safe = jnp.maximum(blocks, 0)
    return jnp.where(blocks >= 0, (safe % tiles) * rows + safe // tiles, -1)


def gather_kernel(pairs, current_ref, blocks_ref, cols_ref, out_ref, parts):
    _, rows, width = current_ref.shape
    tiles = width // LANES
    for j in range(tiles):
        for c in range(2):
            for k, part in enumerate(split3(current_ref[c, :, j * LANES : (j + 1) * LANES])):
                parts[k, j * rows : (j + 1) * rows, c * LANES : (c + 1) * LANES] = part
    lane = lax.broadcasted_iota(jnp.int32, (LANES, LANES), 1)
    for g in range(blocks_ref.shape[0]):
        spread = jnp.broadcast_to(blocks_ref[g : g + 1, :], (LANES, LANES))
        turned = jnp.transpose(spread)
        pick = jnp.concatenate(
            [
                jnp.where(turned == lane + b * LANES, 1.0, 0.0).astype(jnp.bfloat16)
                for b in range(rows * tiles // LANES)
            ],
            axis=1,
        )
        picked = nn_dot(pick, parts[0]) + nn_dot(pick, parts[1]) + nn_dot(pick, parts[2])
        cols = cols_ref[g * LANES : (g + 1) * LANES, :]
        index = jnp.maximum(cols, 0)
        for c in range(2):
            taken = lane_take(picked[:, c * LANES : (c + 1) * LANES], index)
            taken = jnp.where(cols >= 0, taken, 0.0)
            for d in range(LANES // pairs):
                out_ref[g * (LANES // pairs) + d, c] = taken[d * pairs : (d + 1) * pairs]


def inverse_kernel(cols_ref, out_ref):
    lane = lax.broadcasted_iota(jnp.int32, (8, LANES), 1)
    sub = lax.broadcasted_iota(jnp.int32, (8, LANES), 0)
    order = (lane + 1).astype(jnp.float32)
    index = (lane % 16) * 8 + sub
    group = lane // 16

    def body(i, carry):
        at = pl.multiple_of(i * 8, 8)
        cols = cols_ref[pl.ds(at, 8), :]
        high = jnp.right_shift(cols, 4)
        low = jnp.bitwise_and(cols, 15)
        left = jnp.concatenate([jnp.where(high == h, 1.0, 0.0) for h in range(8)], axis=0)
        right = jnp.concatenate([jnp.where(low == b, order, 0.0) for b in range(16)], axis=0)
        product = lax.dot_general(
            left.astype(jnp.bfloat16),
            right.astype(jnp.bfloat16),
            (((1,), (1,)), ((), ())),
            preferred_element_type=jnp.float32,
        )
        found = jnp.zeros((8, LANES), jnp.float32)
        for h in range(8):
            found = jnp.where(group == h, lane_take(product[h * 8 : (h + 1) * 8], index), found)
        out_ref[pl.ds(at, 8), :] = found.astype(jnp.int32) - 1
        return carry

    lax.fori_loop(0, cols_ref.shape[0] // 8, body, 0, unroll=4)


def ice_kernel(mass_ref, coriolis_ref, start_ref, wind_ref, current_ref, velocity_ref, drag_ref):
    devices, pairs, width = mass_ref.shape
    lane = lax.broadcasted_iota(jnp.int32, (pairs, width), 1)
    first, last = lane == 0, lane == width - 1

    def beside(values):
        before = jnp.where(first, 0.0, pltpu.roll(values, 1, 1))
        after = jnp.where(last, 0.0, pltpu.roll(values, width - 1, 1))
        return before + after

    for d in range(devices):
        mass = mass_ref[d]
        diagonal = mass + drag_coeff + 2.0 * link_coeff
        turning = coriolis_ref[d] * mass
        inverse = 1.0 / (diagonal * diagonal + turning * turning)
        diagonal = diagonal * inverse
        turning = turning * inverse
        east, north = start_ref[0, d], start_ref[1, d]
        base_east = mass * east + wind_ref[0, d] + drag_coeff * current_ref[d, 0]
        base_north = mass * north + wind_ref[1, d] + drag_coeff * current_ref[d, 1]
        for _ in range(ICE_SWEEPS):
            right_east = base_east + link_coeff * beside(east)
            right_north = base_north + link_coeff * beside(north)
            east = diagonal * right_east + turning * right_north
            north = diagonal * right_north - turning * right_east
        velocity_ref[0, d] = east
        velocity_ref[1, d] = north
        drag_ref[d, 0] = drag_coeff * (east - current_ref[d, 0])
        drag_ref[d, 1] = drag_coeff * (north - current_ref[d, 1])


def scatter_kernel(pairs, drag_ref, blocks_ref, inverse_ref, out_ref, edge_ref, total):
    _, rows, width = out_ref.shape
    tiles = width // LANES
    count = rows * tiles
    row = lax.broadcasted_iota(jnp.int32, (count, LANES), 0)
    for g in range(blocks_ref.shape[0]):
        put = jnp.where(
            jnp.broadcast_to(blocks_ref[g : g + 1, :], (count, LANES)) == row, 1.0, 0.0
        ).astype(jnp.bfloat16)
        inverse = inverse_ref[g * LANES : (g + 1) * LANES, :]
        index = jnp.maximum(inverse, 0)
        halves = []
        for c in range(2):
            values = jnp.concatenate(
                [drag_ref[g * (LANES // pairs) + d, c] for d in range(LANES // pairs)], axis=0
            )
            halves.append(jnp.where(inverse >= 0, lane_take(values, index), 0.0))
        high, middle, low = split3(jnp.concatenate(halves, axis=1))
        added = nn_dot(put, high) + nn_dot(put, middle) + nn_dot(put, low)
        if g == 0:
            total[...] = added
        else:
            total[...] += added
    for c in range(2):
        for j in range(tiles):
            out_ref[c, :, j * LANES : (j + 1) * LANES] = total[
                j * rows : (j + 1) * rows, c * LANES : (c + 1) * LANES
            ]
    pack_edges([out_ref.at[0], out_ref.at[1]], edge_ref)


def pack_edges(refs, edge_ref):
    rows, width = refs[0].shape
    per = LANES // COL_RIM
    slot = lax.broadcasted_iota(jnp.int32, (rows, LANES), 1) // COL_RIM
    for start in range(0, len(refs), per):
        tile = start // per
        first = jnp.zeros((rows, LANES), jnp.float32)
        last = first
        for k, ref in enumerate(refs[start : start + per]):
            head = ref[:, :LANES]
            tail = ref[:, width - LANES :]
            if k:
                head = pltpu.roll(head, k * COL_RIM, 1)
            if (k + 1) * COL_RIM != LANES:
                tail = pltpu.roll(tail, (k + 1) * COL_RIM, 1)
            first = jnp.where(slot == k, head, first)
            last = jnp.where(slot == k, tail, last)
        edge_ref[0, :, tile * LANES : (tile + 1) * LANES] = first
        edge_ref[1, :, tile * LANES : (tile + 1) * LANES] = last


def prepare_kernel(sea_ref, forcing_ref, weights_ref, excess_ref, mask_ref, out_ref, edge_ref):
    total = weights_ref[0]
    for k in range(1, 8):
        total = total + weights_ref[k]
    ocean = mask_ref[...] > 0
    inverse = jnp.where(ocean, 1.0 / ((1.0 + excess_ref[...]) * total), 0.0)
    for k in range(8):
        out_ref[k] = weights_ref[k] * inverse
    out_ref[8] = inverse
    out_ref[9] = jnp.where(ocean, sea_ref[...], 0.0)
    out_ref[10] = forcing_ref[...]
    pack_edges([out_ref.at[k] for k in range(out_ref.shape[0])], edge_ref)


def widen_kernel(body_ref, east_ref, west_ref, tile_ref, rows_ref):
    arrays, rows, width = body_ref.shape
    per = LANES // COL_RIM
    slot = lax.broadcasted_iota(jnp.int32, (rows, LANES), 1) // COL_RIM
    for k in range(arrays):
        at = (k // per) * LANES
        spot = k % per
        east = east_ref[:, at : at + LANES]
        west = west_ref[:, at : at + LANES]
        if spot:
            east = pltpu.roll(east, LANES - spot * COL_RIM, 1)
        if spot != per - 1:
            west = pltpu.roll(west, LANES - (spot + 1) * COL_RIM, 1)
        tile_ref[k] = jnp.where(slot == 0, east, jnp.where(slot == per - 1, west, 0.0))
        for side, start in ((0, 0), (1, rows - ROW_RIM)):
            rows_ref[side, k, :, :width] = body_ref[k, start : start + ROW_RIM, :]
            rows_ref[side, k, :, width:] = tile_ref[k, start : start + ROW_RIM, :]


def sweep_kernel(
    body_ref, tile_ref, south_ref, north_ref,
    stress_ref, stress_tile_ref, stress_south_ref, stress_north_ref,
    out_ref, field, wide_ref, even_ref, odd_ref,
):
    arrays, rows, width = body_ref.shape
    tall, wide = rows + 2 * ROW_RIM, width + LANES
    half = tall // 2
    tiles = wide // LANES

    def gather_into(k, body, tile, south, north):
        for t in range(tiles):
            at = k * tiles + t
            part = slice(t * LANES, (t + 1) * LANES)
            field[at, :rows, :] = body[:, part] if t < tiles - 1 else tile[...]
            field[at, rows : rows + ROW_RIM, :] = south[:, part]
            field[at, rows + ROW_RIM :, :] = north[:, part]

    for k in range(arrays):
        gather_into(k, body_ref.at[k], tile_ref.at[k], south_ref.at[k], north_ref.at[k])
    for c in range(2):
        for ref, start, size, left, length in (
            (stress_ref, 0, rows, 0, width),
            (stress_tile_ref, 0, rows, width, LANES),
            (stress_south_ref, rows, ROW_RIM, 0, wide),
            (stress_north_ref, rows + ROW_RIM, ROW_RIM, 0, wide),
        ):
            wide_ref[c, start : start + size, left : left + length] = ref[c]
    east_stress = wide_ref[0]
    north_stress = wide_ref[1]
    change = (
        pltpu.roll(north_stress, wide - 1, 1)
        - pltpu.roll(north_stress, 1, 1)
        - pltpu.roll(east_stress, tall - 1, 0)
        + pltpu.roll(east_stress, 1, 0)
    )
    for t in range(tiles):
        part = change[:, t * LANES : (t + 1) * LANES]
        field[10 * tiles + t] = (field[10 * tiles + t] + part) * field[8 * tiles + t]

    even_rows, odd_rows = pl.ds(0, half, stride=2), pl.ds(1, half, stride=2)
    column_odd = lax.broadcasted_iota(jnp.int32, (half, wide), 1) % 2

    def take(k, which):
        return jnp.concatenate([field[k * tiles + t, which, :] for t in range(tiles)], axis=1)

    even_ref[...] = take(9, even_rows)
    odd_ref[...] = take(9, odd_rows)

    def phase(own_ref, other_ref, which, odd, colours):
        base = take(10, which)
        other = other_ref[...]
        if odd:
            above, below = other, pltpu.roll(other, half - 1, 0)
        else:
            above, below = pltpu.roll(other, 1, 0), other
        base = base + take(2, which) * below + take(3, which) * above
        base = base + take(4, which) * pltpu.roll(below, wide - 1, 1)
        base = base + take(5, which) * pltpu.roll(below, 1, 1)
        base = base + take(6, which) * pltpu.roll(above, wide - 1, 1)
        base = base + take(7, which) * pltpu.roll(above, 1, 1)
        own = own_ref[...]
        for parity in colours:
            new = base + take(0, which) * pltpu.roll(own, wide - 1, 1)
            new = new + take(1, which) * pltpu.roll(own, 1, 1)
            own = jnp.where(column_odd == parity, new, own)
        own_ref[...] = own

    runs = [(0, [0, 1])]
    for _ in range(SWEEPS):
        runs += [(1, [0, 1, 0]), (0, [1, 0, 1])]
    runs[-1] = (0, [1, 0])
    for odd, colours in runs:
        if odd:
            phase(odd_ref, even_ref, odd_rows, True, colours)
        else:
            phase(even_ref, odd_ref, even_rows, False, colours)
    for t in range(tiles - 1):
        part = slice(t * LANES, (t + 1) * LANES)
        field[t, pl.ds(0, rows // 2, stride=2), :] = even_ref[: rows // 2, part]
        field[t, pl.ds(1, rows // 2, stride=2), :] = odd_ref[: rows // 2, part]
        out_ref[:, part] = field[t, :rows, :]


def shift(values, axis, step, wrap):
    count = lax.axis_size(axis)
    pairs = [(i, (i + step) % count) for i in range(count) if wrap or 0 <= i + step < count]
    return lax.ppermute(values, axis, pairs)


def widen(body, edge):
    arrays, rows, width = body.shape
    east = shift(edge[0], "zon", -1, True)
    west = shift(edge[1], "zon", 1, True)
    tile, ends = pl.pallas_call(
        widen_kernel,
        out_shape=(
            jax.ShapeDtypeStruct((arrays, rows, LANES), jnp.float32),
            jax.ShapeDtypeStruct((2, arrays, ROW_RIM, width + LANES), jnp.float32),
        ),
        in_specs=[VM] * 3,
        out_specs=(VM, VM),
        compiler_params=PARAMS,
        cost_estimate=cost(arrays * rows * 1024, arrays * rows * 1024),
        name="widen",
    )(body, east, west)
    south = shift(ends[0], "mer", -1, False)
    north = shift(ends[1], "mer", 1, False)
    return tile, south, north


def local(
    sea_level,
    forcing,
    link_weights,
    excess,
    ocean_mask,
    current,
    intersection_block,
    intersection_cols,
    ice_mass,
    coriolis,
    ice_start,
    wind_stress,
):
    rows, width = sea_level.shape
    _, devices, pairs, block = intersection_cols.shape
    slots = devices * pairs
    tiles = width // LANES
    f32 = jnp.float32
    names = ("zon", "mer")
    blocks = block_rows(intersection_block.reshape(slots // LANES, LANES), tiles, rows)
    cols = intersection_cols.reshape(slots, block)
    ice_shape = (devices, pairs, block)
    slot_bytes = slots * block * 4

    values = pl.pallas_call(
        functools.partial(gather_kernel, pairs),
        out_shape=jax.ShapeDtypeStruct((devices, 2, pairs, block), f32),
        in_specs=[VM] * 3,
        out_specs=VM,
        scratch_shapes=[pltpu.VMEM((3, rows * tiles, 2 * LANES), jnp.bfloat16)],
        compiler_params=PARAMS,
        cost_estimate=cost(slots * rows * tiles * 1536, 4 * slot_bytes),
        name="pick",
    )(current, blocks, cols)
    ice_current = lax.all_to_all(values, names, split_axis=0, concat_axis=0, tiled=True)

    inverse = pl.pallas_call(
        inverse_kernel,
        out_shape=jax.ShapeDtypeStruct((slots, block), jnp.int32),
        in_specs=[VM],
        out_specs=VM,
        compiler_params=PARAMS,
        cost_estimate=cost(slots * block * 4096, 4 * slot_bytes),
        name="inverse",
    )(cols)
    arrays = 11
    edge_width = -(-arrays * COL_RIM // LANES) * LANES
    body, edge = pl.pallas_call(
        prepare_kernel,
        out_shape=(
            jax.ShapeDtypeStruct((arrays, rows, width), f32),
            jax.ShapeDtypeStruct((2, rows, edge_width), f32),
        ),
        in_specs=[VM] * 5,
        out_specs=(VM, VM),
        compiler_params=PARAMS,
        cost_estimate=cost(rows * width * 64, rows * width * 96),
        name="prepare",
    )(sea_level, forcing, link_weights, excess, ocean_mask)
    tile, south, north = widen(body, edge)

    steps = 4
    part = devices // steps
    one = pl.BlockSpec((part, pairs, block), lambda i: (i, 0, 0))
    two = pl.BlockSpec((2, part, pairs, block), lambda i: (0, i, 0, 0))
    turned = pl.BlockSpec((part, 2, pairs, block), lambda i: (i, 0, 0, 0))
    velocity, drag = pl.pallas_call(
        ice_kernel,
        grid=(steps,),
        out_shape=(
            jax.ShapeDtypeStruct((2,) + ice_shape, f32),
            jax.ShapeDtypeStruct((devices, 2, pairs, block), f32),
        ),
        in_specs=[one, one, two, two, turned],
        out_specs=(two, turned),
        compiler_params=PARAMS,
        cost_estimate=cost(slots * block * 80, 12 * slot_bytes),
        name="ice",
    )(
        ice_mass.reshape(ice_shape),
        coriolis.reshape(ice_shape),
        ice_start.reshape((2,) + ice_shape),
        wind_stress.reshape((2,) + ice_shape),
        ice_current,
    )
    returned = lax.all_to_all(drag, names, split_axis=0, concat_axis=0, tiled=True)

    stress, stress_edge = pl.pallas_call(
        functools.partial(scatter_kernel, pairs),
        out_shape=(
            jax.ShapeDtypeStruct((2, rows, width), f32),
            jax.ShapeDtypeStruct((2, rows, LANES), f32),
        ),
        in_specs=[VM] * 3,
        out_specs=(VM, VM),
        scratch_shapes=[pltpu.VMEM((rows * tiles, 2 * LANES), f32)],
        compiler_params=PARAMS,
        cost_estimate=cost(slots * rows * tiles * 1536, 4 * slot_bytes),
        name="put",
    )(returned, blocks, inverse)
    stress_tile, stress_south, stress_north = widen(stress, stress_edge)

    tall, wide = rows + 2 * ROW_RIM, width + LANES
    surface = pl.pallas_call(
        sweep_kernel,
        out_shape=jax.ShapeDtypeStruct((rows, width), f32),
        in_specs=[VM] * 8,
        out_specs=VM,
        scratch_shapes=[
            pltpu.VMEM((arrays * (wide // LANES), tall, LANES), f32),
            pltpu.VMEM((2, tall, wide), f32),
            pltpu.VMEM((tall // 2, wide), f32),
            pltpu.VMEM((tall // 2, wide), f32),
        ],
        compiler_params=PARAMS,
        cost_estimate=cost(rows * width * 200, rows * width * 64),
        name="sweep",
    )(body, tile, south, north, stress, stress_tile, stress_south, stress_north)
    return (surface, velocity.reshape((2, 1) + ice_shape))


def solution(mesh):
    return jax.shard_map(
        local,
        mesh=mesh,
        in_specs=(
            P("mer", "zon"),
            P("mer", "zon"),
            P(None, "mer", "zon"),
            P("mer", "zon"),
            P("mer", "zon"),
            P(None, "mer", "zon"),
            P(("zon", "mer"), None, None),
            P(("zon", "mer"), None, None, None),
            P(("zon", "mer"), None, None, None),
            P(("zon", "mer"), None, None, None),
            P(None, ("zon", "mer"), None, None, None),
            P(None, ("zon", "mer"), None, None, None),
        ),
        out_specs=(P("mer", "zon"), P(None, ("zon", "mer"), None, None, None)),
        check_vma=False,
    )
```

time: 1460 us -> 105 us (0.07)
  other arithmetic: 753 us -> 1.55 us
  local copies, waits for them, and re-layouts: 607 us -> 10.2 us
  waiting for transfers between devices: 50.3 us -> 9.06 us
  blocking collectives: 0 us -> 32.1 us
  Pallas kernels: 0 us -> 26.2 us
  starting transfers between devices: 41.2 us -> 24.7 us
    scatter-add x1 -> x0, other arithmetic: 707 us -> none  [local(): jnp.zeros((2, cell_count), jnp.float32).at[:, flat_target]]
    gather x2 -> x0, local copies, waits for them, and re-layouts: 481 us -> none  [local(): jnp.take(flat_current, jnp.minimum(flat_target, cell_count - 1), axis=1)]
    slice x7 -> x0, local copies, waits for them, and re-layouts: 48.6 us -> none  [the longest x1 34.7 us: local(): cycle_north = padded_2(stress_grid[1], (('zon', 1),), 1, True)]
    all_to_all x2 -> x1, waiting for transfers between devices: 44.8 us -> 0.41 us  [local(): lax.all_to_all(drag, names, split_axis=0, concat_axis=0, tiled=True)]
    another operation x2 -> x0, local copies, waits for them, and re-layouts: 33 us -> none  [local(): returned = to_ocean(ice_drag)[:, 0].reshape(2, slot_count * block)]
    all_to_all x0 -> x1, blocking collectives: none -> 32.1 us  [local(): lax.all_to_all(values, names, split_axis=0, concat_axis=0, tiled=True)]
    pallas_call x0 -> x8, Pallas kernels: none -> 26.2 us  [the longest x1 8.98 us: local(): pl.pallas_call(inverse_kernel, out_shape=jax.ShapeDtypeStruct((slots, blo...]
    select_n x16 -> x1, other arithmetic: 24.5 us -> 0.01 us  [block_rows(): return jnp.where(blocks >= 0, safe % tiles * rows + safe // tiles, -1)]
  transfers between devices with their start and end apart: 10 -> 9, of which waited for: 4 -> 3; matrix products, arithmetic and copies ran while one was open for 2% -> 0% of each run, Pallas kernels for 0% -> 11%
where the time goes in v1:
time: 105 us
  blocking collectives  32.1 us (31%)
  Pallas kernels  26.2 us (25%)
  starting transfers between devices  24.7 us (24%)
  local copies, waits for them, and re-layouts  10.2 us (10%)
  waiting for transfers between devices  9.06 us (9%)
  other arithmetic  1.55 us (1%)
    all_to_all x1, blocking collectives, local(): lax.all_to_all(values, names, split_axis=0, concat_axis=0, tiled=True)  32.1 us
    ppermute x8, starting transfers between devices, shift(): return lax.ppermute(values, axis, pairs)  20 us
    unnamed x36, local copies, waits for them, and re-layouts  9.83 us
    pallas_call x1, Pallas kernels, local(): pl.pallas_call(inverse_kernel, out_shape=jax.ShapeDtypeStruct((slots, blo...  8.98 us
    ppermute x8, waiting for transfers between devices, shift(): return lax.ppermute(values, axis, pairs)  8.65 us
    pallas_call x1, Pallas kernels, local(): pl.pallas_call(ice_kernel, grid=(steps,), out_shape=(jax.ShapeDtypeStruct...  5.36 us
    all_to_all x1, starting transfers between devices, local(): lax.all_to_all(drag, names, split_axis=0, concat_axis=0, tiled=True)  4.68 us
    pallas_call x1, Pallas kernels, local(): pl.pallas_call(sweep_kernel, out_shape=jax.ShapeDtypeStruct((rows, width)...  4.46 us
  transfers between devices with their start and end apart: 9, of which 3 were waited for; matrix products, arithmetic and copies ran while one was open for 0% of the time, Pallas kernels for 11%

profile of v1, /device:TPU:1, one launch (start us, length us, event | category | flops | bytes accessed | tf_op | source)
XLA Modules:
  0.0 104.7 jit_solution(9524353761570903839)
XLA Ops:
  0.6 0.0 copy-start.3
  0.6 0.8 sign_compare_fusion
  1.5 0.7 maximum_shift-right-logical_fusion
  2.2 0.1 ne.26
  2.3 0.1 ge.7
  2.4 0.1 div.12
  2.4 0.1 rem.18
  2.5 0.0 copy-start.13
  2.5 1.2 %copy-done.13 = f32[2,128,512]{2,1,0:T(8,128)S(1)} copy-done((f32[2,128,512]{2,1,0:T(8,128)S(1)}, f32[2,128,512]{2,1,0:T(8,128)}, u32[]{:S(2)}) %copy-start.13) | copy-done | bytes 524312
  3.7 1.0 copy-done.14
  4.8 1.3 %pick.1 = f32[32,2,32,128]{3,2,1,0:T(8,128)S(1)} custom-call(f32[2,128,512]{2,1,0:T(8,128)S(1)} %copy-done.13, s32[8,128]{1,0:T(8,128)S(1)} %fusion.2.blocks_ref, s32[1024,128]{1,0:T(8,128)S(1)} %bitcast.28), custom_call_target="tpu_custom_call" | custom-call | flops 805306368 | bytes 2097152 | tf_op jit(solution)/shard_map/pick/pallas_call | solution.py:356
  6.0 32.1 %all_to_all.10.current_ref = f32[32,2,32,128]{3,2,1,0:T(8,128)S(1)} all-to-all(f32[32,2,32,128]{3,2,1,0:T(8,128)S(1)} %pick.1), channel_id=1, replica_groups=mesh['zon'=8,'mer'=4] {'zon','mer'}, dimensions={0} | all-to-all | bytes 2097152 | tf_op jit(solution)/shard_map/all_to_all | solution.py:366
  38.1 0.0 copy-done.7
  38.1 0.0 copy-start.2
  38.1 0.0 copy-start.9
  38.2 5.4 %ice.1 = (f32[2,32,32,128]{3,2,1,0:T(8,128)}, f32[32,2,32,128]{3,2,1,0:T(8,128)}) custom-call(f32[32,32,128]{2,1,0:T(8,128)S(1)} %bitcast.26, f32[32,32,128]{2,1,0:T(8,128)S(1)} %bitcast.27, f32[2,32,32,128]{3,2,1,0:T(8,128)S(1)} %bitcast.24, f32[2,32,32,128]{3,2,1,0:T(8,128)S(1)} %bitcast.25, f32[32,2,32,128]{3,2,1,0:T(8,128)S(1)} %all_to_all.10.current_ref), custom_call_target="tpu_custom_call" | custom-call | flops 10485760 | bytes 6291456 | tf_op jit(solution)/shard_map/ice/pallas_call | solution.py:398
  43.5 4.7 %all-to-all-start.1 = ((f32[32,2,32,128]{3,2,1,0:T(8,128)}), f32[32,2,32,128]{3,2,1,0:T(8,128)}, u32[]{:S(2)}, u32[]{:S(2)}) async-start(f32[32,2,32,128]{3,2,1,0:T(8,128)} %get-tuple-element.16), calls=%async_computation.1 | async-start | bytes 2097152 | tf_op jit(solution)/shard_map/all_to_all | solution.py:417
  48.2 0.0 copy-start.10
  48.2 0.9 copy-done.10
  49.2 0.9 copy-done.11
  50.1 0.9 copy-done.12
  51.1 2.3 %prepare.1 = (f32[11,128,512]{2,1,0:T(8,128)}, f32[2,128,256]{2,1,0:T(8,128)S(1)}) custom-call(f32[128,512]{1,0:T(8,128)S(1)} %copy-done.9, f32[128,512]{1,0:T(8,128)S(1)} %copy-done.10, f32[8,128,512]{2,1,0:T(8,128)S(1)} %copy-done.2, f32[128,512]{1,0:T(8,128)S(1)} %copy-done.11, s32[128,512]{1,0:T(8,128)S(1)} %copy-done.12), custom_call_target="tpu_custom_call" | custom-call | flops 4194304 | bytes 6291456 | tf_op jit(solution)/shard_map/prepare/pallas_call | solution.py:379
  53.4 1.4 %collective-permute-start.1 = (f32[128,256]{1,0:T(8,128)S(1)}, f32[128,256]{1,0:T(8,128)S(1)}, u32[]{:S(2)}, u32[]{:S(2)}) collective-permute-start(f32[128,256]{1,0:T(8,128)S(1)} %get-tuple-element.26), channel_id=1, source_target_pairs={{0,4},{4,8},{8,12},{12,16},{16,20},{20,24},{24,28},{28,0},{1,5},{5... | collective-permute-start | bytes 393224 | tf_op jit(solution)/shard_map/ppermute | solution.py:307
  54.8 2.9 %collective-permute-start = (f32[128,256]{1,0:T(8,128)S(1)}, f32[128,256]{1,0:T(8,128)S(1)}, u32[]{:S(2)}, u32[]{:S(2)}) collective-permute-start(f32[128,256]{1,0:T(8,128)S(1)} %get-tuple-element.27), channel_id=1, source_target_pairs={{0,28},{4,0},{8,4},{12,8},{16,12},{20,16},{24,20},{28,24},{1,29},{... | collective-permute-start | bytes 393224 | tf_op jit(solution)/shard_map/ppermute | solution.py:307
  57.7 9.0 %inverse.1.inverse_ref = s32[1024,128]{1,0:T(8,128)S(1)} custom-call(s32[1024,128]{1,0:T(8,128)S(1)} %bitcast.29), custom_call_target="tpu_custom_call" | custom-call | flops 536870912 | bytes 2097152 | tf_op jit(solution)/shard_map/inverse/pallas_call | solution.py:368
  66.7 0.8 copy-done.16
  67.5 5.3 %collective-permute-done.1.west_ref = f32[128,256]{1,0:T(8,128)S(1)} collective-permute-done((f32[128,256]{1,0:T(8,128)S(1)}, f32[128,256]{1,0:T(8,128)S(1)}, u32[]{:S(2)}, u32[]{:S(2)}) %collective-permute-start.1) | collective-permute-done | bytes 131104 | tf_op jit(solution)/shard_map/ppermute | solution.py:307
  72.7 0.0 collective-permute-done.east_ref
  72.7 1.8 %copy-done = f32[11,128,512]{2,1,0:T(8,128)S(1)} copy-done((f32[11,128,512]{2,1,0:T(8,128)S(1)}, f32[11,128,512]{2,1,0:T(8,128)}, u32[]{:S(2)}) %copy-start) | copy-done | bytes 2883608
  74.5 0.4 widen.2
  75.0 0.9 copy-done.5
  75.8 0.4 all-to-all-done.1.drag_ref
  76.2 1.2 %copy-done.17 = s32[1024,128]{1,0:T(8,128)S(1)} copy-done((s32[1024,128]{1,0:T(8,128)S(1)}, s32[1024,128]{1,0:T(8,128)}, u32[]{:S(2)}) %copy-start.17) | copy-done | bytes 524312
  77.5 3.4 %put.1 = (f32[2,128,512]{2,1,0:T(8,128)S(1)}, f32[2,128,128]{2,1,0:T(8,128)S(1)}) custom-call(f32[32,2,32,128]{3,2,1,0:T(8,128)} %all-to-all-done.1.drag_ref, s32[8,128]{1,0:T(8,128)S(1)} %fusion.2.blocks_ref, s32[1024,128]{1,0:T(8,128)S(1)} %copy-done.17), custom_call_target="tpu_custom_call" | custom-call | flops 805306368 | bytes 2097152 | tf_op jit(solution)/shard_map/put/pallas_call | solution.py:419
  80.9 1.1 %collective-permute-start.5 = (f32[128,128]{1,0:T(8,128)S(1)}, f32[128,128]{1,0:T(8,128)S(1)}, u32[]{:S(2)}, u32[]{:S(2)}) collective-permute-start(f32[128,128]{1,0:T(8,128)S(1)} %get-tuple-element.28), channel_id=1, source_target_pairs={{0,4},{4,8},{8,12},{12,16},{16,20},{20,24},{24,28},{28,0},{1,5},{5... | collective-permute-start | bytes 196616 | tf_op jit(solution)/shard_map/ppermute | solution.py:307
  82.0 3.1 %collective-permute-start.4 = (f32[128,128]{1,0:T(8,128)S(1)}, f32[128,128]{1,0:T(8,128)S(1)}, u32[]{:S(2)}, u32[]{:S(2)}) collective-permute-start(f32[128,128]{1,0:T(8,128)S(1)} %get-tuple-element.29), channel_id=1, source_target_pairs={{0,28},{4,0},{8,4},{12,8},{16,12},{20,16},{24,20},{28,24},{1,29},{... | collective-permute-start | bytes 196616 | tf_op jit(solution)/shard_map/ppermute | solution.py:307
  85.1 4.1 %collective-permute-start.3 = (f32[11,8,640]{2,1,0:T(8,128)S(1)}, f32[11,8,640]{2,1,0:T(8,128)S(1)}, u32[]{:S(2)}, u32[]{:S(2)}) collective-permute-start(f32[11,8,640]{2,1,0:T(8,128)S(1)} %get-tuple-element.24), channel_id=1, source_target_pairs={{0,1},{1,2},{2,3},{4,5},{5,6},{6,7},{8,9},{9,10},{10,11},{12,13},{... | collective-permute-start | bytes 675848 | tf_op jit(solution)/shard_map/ppermute | solution.py:307
  89.2 1.9 %collective-permute-start.2 = (f32[11,8,640]{2,1,0:T(8,128)S(1)}, f32[11,8,640]{2,1,0:T(8,128)S(1)}, u32[]{:S(2)}, u32[]{:S(2)}) collective-permute-start(f32[11,8,640]{2,1,0:T(8,128)S(1)} %get-tuple-element.25), channel_id=1, source_target_pairs={{1,0},{2,1},{3,2},{5,4},{6,5},{7,6},{9,8},{10,9},{11,10},{13,12},{... | collective-permute-start | bytes 675848 | tf_op jit(solution)/shard_map/ppermute | solution.py:307
  91.1 0.0 collective-permute-done.5.west_ref
  91.1 0.0 collective-permute-done.4.east_ref
  91.1 0.1 widen.3
  91.3 3.6 %collective-permute-start.7 = (f32[2,8,640]{2,1,0:T(8,128)S(1)}, f32[2,8,640]{2,1,0:T(8,128)S(1)}, u32[]{:S(2)}, u32[]{:S(2)}) collective-permute-start(f32[2,8,640]{2,1,0:T(8,128)S(1)} %get-tuple-element.30), channel_id=1, source_target_pairs={{0,1},{1,2},{2,3},{4,5},{5,6},{6,7},{8,9},{9,10},{10,11},{12,13},{... | collective-permute-start | bytes 122888 | tf_op jit(solution)/shard_map/ppermute | solution.py:307
  94.9 1.9 %collective-permute-start.6 = (f32[2,8,640]{2,1,0:T(8,128)S(1)}, f32[2,8,640]{2,1,0:T(8,128)S(1)}, u32[]{:S(2)}, u32[]{:S(2)}) collective-permute-start(f32[2,8,640]{2,1,0:T(8,128)S(1)} %get-tuple-element.31), channel_id=1, source_target_pairs={{1,0},{2,1},{3,2},{5,4},{6,5},{7,6},{9,8},{10,9},{11,10},{13,12},{... | collective-permute-start | bytes 122888 | tf_op jit(solution)/shard_map/ppermute | solution.py:307
  96.9 0.0 collective-permute-done.3.north_ref
  96.9 0.0 collective-permute-done.2.south_ref
  96.9 0.0 collective-permute-done.7.stress_north_ref
  96.9 3.4 %collective-permute-done.6.stress_south_ref = f32[2,8,640]{2,1,0:T(8,128)S(1)} collective-permute-done((f32[2,8,640]{2,1,0:T(8,128)S(1)}, f32[2,8,640]{2,1,0:T(8,128)S(1)}, u32[]{:S(2)}, u32[]{:S(2)}) %collective-permute-start.6) | collective-permute-done | bytes 40992 | tf_op jit(solution)/shard_map/ppermute | solution.py:307
  100.3 4.5 %sweep.1 = f32[128,512]{1,0:T(8,128)} custom-call(f32[11,128,512]{2,1,0:T(8,128)S(1)} %copy-done.1, f32[11,128,128]{2,1,0:T(8,128)S(1)} %copy-done.6, f32[11,8,640]{2,1,0:T(8,128)S(1)} %collective-permute-done.2.south_ref, f32[11,8,640]{2,1,0:T(8,128)S(1)} %collective-permute-done.3.north_ref, f32[2,128,512]{2,1,0:T(8,128)S(1)} %get-tuple-element.17.body_ref.stress_ref, ...), custom_call_target="tpu_custom_call" | custom-call | flops 13107200 | bytes 4194304 | tf_op jit(solution)/shard_map/sweep/pallas_call | solution.py:435
  (26 shorter events, 0.1 us)
Async XLA Ops:
  0.6 37.5 %copy-start.3 = (f32[2,1,32,32,128]{4,3,2,1,0:T(8,128)S(1)}, f32[2,1,32,32,128]{4,3,2,1,0:T(8,128)}, u32[]{:S(2)}) copy-start(f32[2,1,32,32,128]{4,3,2,1,0:T(8,128)} %param.22) | copy-start | bytes 3145732
  2.5 35.6 %copy-start.4 = (f32[2,1,32,32,128]{4,3,2,1,0:T(8,128)S(1)}, f32[2,1,32,32,128]{4,3,2,1,0:T(8,128)}, u32[]{:S(2)}) copy-start(f32[2,1,32,32,128]{4,3,2,1,0:T(8,128)} %param.23) | copy-start | bytes 3145732
  2.5 35.6 %copy-start.7 = (f32[1,32,32,128]{3,2,1,0:T(8,128)S(1)}, f32[1,32,32,128]{3,2,1,0:T(8,128)}, u32[]{:S(2)}) copy-start(f32[1,32,32,128]{3,2,1,0:T(8,128)} %param.20) | copy-start | bytes 1572868
  2.5 35.6 %copy-start.8 = (f32[1,32,32,128]{3,2,1,0:T(8,128)S(1)}, f32[1,32,32,128]{3,2,1,0:T(8,128)}, u32[]{:S(2)}) copy-start(f32[1,32,32,128]{3,2,1,0:T(8,128)} %param.21) | copy-start | bytes 1572868
  2.5 1.2 %copy-start.13 = (f32[2,128,512]{2,1,0:T(8,128)S(1)}, f32[2,128,512]{2,1,0:T(8,128)}, u32[]{:S(2)}) copy-start(f32[2,128,512]{2,1,0:T(8,128)} %current_ref.1) | copy-start | bytes 1572868
  3.7 1.0 copy-start.14
  38.1 10.1 %copy-start.2 = (f32[8,128,512]{2,1,0:T(8,128)S(1)}, f32[8,128,512]{2,1,0:T(8,128)}, u32[]{:S(2)}) copy-start(f32[8,128,512]{2,1,0:T(8,128)} %weights_ref.1) | copy-start | bytes 6291460
  38.1 10.1 %copy-start.9 = (f32[128,512]{1,0:T(8,128)S(1)}, f32[128,512]{1,0:T(8,128)}, u32[]{:S(2)}) copy-start(f32[128,512]{1,0:T(8,128)} %sea_ref.1) | copy-start | bytes 786436
  43.5 32.7 %all-to-all-start.1 = ((f32[32,2,32,128]{3,2,1,0:T(8,128)}), f32[32,2,32,128]{3,2,1,0:T(8,128)}, u32[]{:S(2)}, u32[]{:S(2)}) async-start(f32[32,2,32,128]{3,2,1,0:T(8,128)} %get-tuple-element.16), calls=%async_computation.1 | async-start | bytes 2097152 | tf_op jit(solution)/shard_map/all_to_all | solution.py:417
  48.2 1.0 copy-start.10
  49.2 0.9 copy-start.11
  50.1 0.9 copy-start.12
  51.1 6.6 %copy-start.15 = (s32[1,32,32,128]{3,2,1,0:T(8,128)S(1)}, s32[1,32,32,128]{3,2,1,0:T(8,128)}, u32[]{:S(2)}) copy-start(s32[1,32,32,128]{3,2,1,0:T(8,128)} %param.19) | copy-start | bytes 1572868
  53.4 19.3 %collective-permute-start.1 = (f32[128,256]{1,0:T(8,128)S(1)}, f32[128,256]{1,0:T(8,128)S(1)}, u32[]{:S(2)}, u32[]{:S(2)}) collective-permute-start(f32[128,256]{1,0:T(8,128)S(1)} %get-tuple-element.26), channel_id=1, source_target_pairs={{0,4},{4,8},{8,12},{12,16},{16,20},{20,24},{24,28},{28,0},{1,5},{5... | collective-permute-start | bytes 393224 | tf_op jit(solution)/shard_map/ppermute | solution.py:307
  54.8 17.9 %collective-permute-start = (f32[128,256]{1,0:T(8,128)S(1)}, f32[128,256]{1,0:T(8,128)S(1)}, u32[]{:S(2)}, u32[]{:S(2)}) collective-permute-start(f32[128,256]{1,0:T(8,128)S(1)} %get-tuple-element.27), channel_id=1, source_target_pairs={{0,28},{4,0},{8,4},{12,8},{16,12},{20,16},{24,20},{28,24},{1,29},{... | collective-permute-start | bytes 393224 | tf_op jit(solution)/shard_map/ppermute | solution.py:307
  66.6 0.8 copy-start.16
  72.7 1.8 %copy-start = (f32[11,128,512]{2,1,0:T(8,128)S(1)}, f32[11,128,512]{2,1,0:T(8,128)}, u32[]{:S(2)}) copy-start(f32[11,128,512]{2,1,0:T(8,128)} %get-tuple-element.12.body_ref) | copy-start | bytes 8650756
  74.9 0.9 copy-start.5
  75.8 24.4 %copy-start.1 = (f32[11,128,512]{2,1,0:T(8,128)S(1)}, f32[11,128,512]{2,1,0:T(8,128)}, u32[]{:S(2)}) copy-start(f32[11,128,512]{2,1,0:T(8,128)} %get-tuple-element.12.body_ref) | copy-start | bytes 8650756
  76.2 1.2 %copy-start.17 = (s32[1024,128]{1,0:T(8,128)S(1)}, s32[1024,128]{1,0:T(8,128)}, u32[]{:S(2)}) copy-start(s32[1024,128]{1,0:T(8,128)} %copy-done.16) | copy-start | bytes 1572868
  77.5 22.8 %copy-start.6 = (f32[11,128,128]{2,1,0:T(8,128)S(1)}, f32[11,128,128]{2,1,0:T(8,128)}, u32[]{:S(2)}) copy-start(f32[11,128,128]{2,1,0:T(8,128)} %copy-done.5) | copy-start | bytes 2162692
  80.9 10.3 %collective-permute-start.5 = (f32[128,128]{1,0:T(8,128)S(1)}, f32[128,128]{1,0:T(8,128)S(1)}, u32[]{:S(2)}, u32[]{:S(2)}) collective-permute-start(f32[128,128]{1,0:T(8,128)S(1)} %get-tuple-element.28), channel_id=1, source_target_pairs={{0,4},{4,8},{8,12},{12,16},{16,20},{20,24},{24,28},{28,0},{1,5},{5... | collective-permute-start | bytes 196616 | tf_op jit(solution)/shard_map/ppermute | solution.py:307
  82.0 9.2 %collective-permute-start.4 = (f32[128,128]{1,0:T(8,128)S(1)}, f32[128,128]{1,0:T(8,128)S(1)}, u32[]{:S(2)}, u32[]{:S(2)}) collective-permute-start(f32[128,128]{1,0:T(8,128)S(1)} %get-tuple-element.29), channel_id=1, source_target_pairs={{0,28},{4,0},{8,4},{12,8},{16,12},{20,16},{24,20},{28,24},{1,29},{... | collective-permute-start | bytes 196616 | tf_op jit(solution)/shard_map/ppermute | solution.py:307
  85.1 11.7 %collective-permute-start.3 = (f32[11,8,640]{2,1,0:T(8,128)S(1)}, f32[11,8,640]{2,1,0:T(8,128)S(1)}, u32[]{:S(2)}, u32[]{:S(2)}) collective-permute-start(f32[11,8,640]{2,1,0:T(8,128)S(1)} %get-tuple-element.24), channel_id=1, source_target_pairs={{0,1},{1,2},{2,3},{4,5},{5,6},{6,7},{8,9},{9,10},{10,11},{12,13},{... | collective-permute-start | bytes 675848 | tf_op jit(solution)/shard_map/ppermute | solution.py:307
  89.2 7.7 %collective-permute-start.2 = (f32[11,8,640]{2,1,0:T(8,128)S(1)}, f32[11,8,640]{2,1,0:T(8,128)S(1)}, u32[]{:S(2)}, u32[]{:S(2)}) collective-permute-start(f32[11,8,640]{2,1,0:T(8,128)S(1)} %get-tuple-element.25), channel_id=1, source_target_pairs={{1,0},{2,1},{3,2},{5,4},{6,5},{7,6},{9,8},{10,9},{11,10},{13,12},{... | collective-permute-start | bytes 675848 | tf_op jit(solution)/shard_map/ppermute | solution.py:307
  91.3 5.6 %collective-permute-start.7 = (f32[2,8,640]{2,1,0:T(8,128)S(1)}, f32[2,8,640]{2,1,0:T(8,128)S(1)}, u32[]{:S(2)}, u32[]{:S(2)}) collective-permute-start(f32[2,8,640]{2,1,0:T(8,128)S(1)} %get-tuple-element.30), channel_id=1, source_target_pairs={{0,1},{1,2},{2,3},{4,5},{5,6},{6,7},{8,9},{9,10},{10,11},{12,13},{... | collective-permute-start | bytes 122888 | tf_op jit(solution)/shard_map/ppermute | solution.py:307
  94.9 5.3 %collective-permute-start.6 = (f32[2,8,640]{2,1,0:T(8,128)S(1)}, f32[2,8,640]{2,1,0:T(8,128)S(1)}, u32[]{:S(2)}, u32[]{:S(2)}) collective-permute-start(f32[2,8,640]{2,1,0:T(8,128)S(1)} %get-tuple-element.31), channel_id=1, source_target_pairs={{1,0},{2,1},{3,2},{5,4},{6,5},{7,6},{9,8},{10,9},{11,10},{13,12},{... | collective-permute-start | bytes 122888 | tf_op jit(solution)/shard_map/ppermute | solution.py:307

commit v2 on v1

--- a/solution.py
+++ b/solution.py
@@ -72,7 +72,7 @@
                 out_ref[g * (LANES // pairs) + d, c] = taken[d * pairs : (d + 1) * pairs]
 
 
-def inverse_kernel(cols_ref, out_ref):
+def inverse_kernel(cols_ref, out_ref, last, back_copy):
     lane = lax.broadcasted_iota(jnp.int32, (8, LANES), 1)
     sub = lax.broadcasted_iota(jnp.int32, (8, LANES), 0)
     order = (lane + 1).astype(jnp.float32)
@@ -98,11 +98,13 @@
         out_ref[pl.ds(at, 8), :] = found.astype(jnp.int32) - 1
         return carry
 
-    lax.fori_loop(0, cols_ref.shape[0] // 8, body, 0, unroll=4)
-
-
-def ice_kernel(mass_ref, coriolis_ref, start_ref, wind_ref, current_ref, velocity_ref, drag_ref):
-    devices, pairs, width = mass_ref.shape
+    lax.fori_loop(0, 1, body, 0)
+    back_copy(last).start()
+    lax.fori_loop(1, cols_ref.shape[0] // 8, body, 0)
+
+
+def ice_block(mass, coriolis, start, wind, current):
+    pairs, width = mass.shape
     lane = lax.broadcasted_iota(jnp.int32, (pairs, width), 1)
     first, last = lane == 0, lane == width - 1
 
@@ -111,25 +113,167 @@
         after = jnp.where(last, 0.0, pltpu.roll(values, width - 1, 1))
         return before + after
 
-    for d in range(devices):
-        mass = mass_ref[d]
-        diagonal = mass + drag_coeff + 2.0 * link_coeff
-        turning = coriolis_ref[d] * mass
-        inverse = 1.0 / (diagonal * diagonal + turning * turning)
-        diagonal = diagonal * inverse
-        turning = turning * inverse
-        east, north = start_ref[0, d], start_ref[1, d]
-        base_east = mass * east + wind_ref[0, d] + drag_coeff * current_ref[d, 0]
-        base_north = mass * north + wind_ref[1, d] + drag_coeff * current_ref[d, 1]
-        for _ in range(ICE_SWEEPS):
-            right_east = base_east + link_coeff * beside(east)
-            right_north = base_north + link_coeff * beside(north)
-            east = diagonal * right_east + turning * right_north
-            north = diagonal * right_north - turning * right_east
-        velocity_ref[0, d] = east
-        velocity_ref[1, d] = north
-        drag_ref[d, 0] = drag_coeff * (east - current_ref[d, 0])
-        drag_ref[d, 1] = drag_coeff * (north - current_ref[d, 1])
+    diagonal = mass + drag_coeff + 2.0 * link_coeff
+    turning = coriolis * mass
+    inverse = 1.0 / (diagonal * diagonal + turning * turning)
+    diagonal = diagonal * inverse
+    turning = turning * inverse
+    east, north = start
+    base_east = mass * east + wind[0] + drag_coeff * current[0]
+    base_north = mass * north + wind[1] + drag_coeff * current[1]
+    for _ in range(ICE_SWEEPS):
+        right_east = base_east + link_coeff * beside(east)
+        right_north = base_north + link_coeff * beside(north)
+        east = diagonal * right_east + turning * right_north
+        north = diagonal * right_north - turning * right_east
+    return east, north
+
+
+def around(sizes, body_ref, edge_ref, east_ref, west_ref, south_ref, north_ref, send, recv):
+    rows = body_ref.shape[1]
+    nz, nm = sizes
+    z, m = lax.axis_index("zon"), lax.axis_index("mer")
+    top, end = pl.ds(0, ROW_RIM), pl.ds(rows - ROW_RIM, ROW_RIM)
+    whole, after, before = pl.ds(0, rows), pl.ds(rows, ROW_RIM), pl.ds(rows + ROW_RIM, ROW_RIM)
+    moves = [
+        (edge_ref.at[0], east_ref.at[whole], -1, 0),
+        (edge_ref.at[1], west_ref.at[whole], 1, 0),
+        (body_ref.at[:, top], south_ref, 0, -1),
+        (body_ref.at[:, end], north_ref, 0, 1),
+        (edge_ref.at[0, top], east_ref.at[after], -1, -1),
+        (edge_ref.at[0, end], east_ref.at[before], -1, 1),
+        (edge_ref.at[1, top], west_ref.at[after], 1, -1),
+        (edge_ref.at[1, end], west_ref.at[before], 1, 1),
+    ]
+    return [
+        pltpu.make_async_remote_copy(
+            src_ref=source,
+            dst_ref=target,
+            send_sem=send.at[i],
+            recv_sem=recv.at[i],
+            device_id={"zon": lax.rem(z + dz + nz, nz), "mer": lax.rem(m + dm + nm, nm)},
+            device_id_type=pl.DeviceIdType.MESH,
+        )
+        for i, (source, target, dz, dm) in enumerate(moves)
+    ]
+
+
+def travel_kernel(
+    sizes,
+    values_ref, mass_ref, coriolis_ref, start_ref, wind_ref,
+    sea_ref, forcing_ref, weights_ref, excess_ref, mask_ref, cols_ref,
+    velocity_ref, returned_ref, inverse_ref, body_ref, east_ref, west_ref, south_ref, north_ref,
+    arrived, drag, edge, send_out, recv_out, send_back, recv_back, send_rim, recv_rim,
+):
+    nz, nm = sizes
+    count = nz * nm
+    z, m = lax.axis_index("zon"), lax.axis_index("mer")
+    me = z * nm + m
+
+    def offsets(k):
+        i = k // nm
+        return nz // 2 + ((i + 1) // 2) * (1 - 2 * (i % 2)), nm - 1 - k % nm
+
+    def ahead(k):
+        dz, dm = offsets(k)
+        return lax.rem(z + dz, nz), lax.rem(m + dm, nm)
+
+    def behind(k):
+        dz, dm = offsets(k)
+        return lax.rem(z - dz + nz, nz), lax.rem(m - dm + nm, nm)
+
+    def out_copy(k):
+        pz, pm = ahead(k)
+        return pltpu.make_async_remote_copy(
+            src_ref=values_ref.at[pz * nm + pm],
+            dst_ref=arrived.at[me],
+            send_sem=send_out.at[k],
+            recv_sem=recv_out.at[k],
+            device_id={"zon": pz, "mer": pm},
+            device_id_type=pl.DeviceIdType.MESH,
+        )
+
+    def back_copy(k):
+        pz, pm = behind(k)
+        return pltpu.make_async_remote_copy(
+            src_ref=drag.at[k],
+            dst_ref=returned_ref.at[me],
+            send_sem=send_back.at[k],
+            recv_sem=recv_back.at[k],
+            device_id={"zon": pz, "mer": pm},
+            device_id_type=pl.DeviceIdType.MESH,
+        )
+
+    barrier = pltpu.get_barrier_semaphore()
+
+    def greet(k, carry):
+        pz, pm = ahead(k)
+        pl.semaphore_signal(
+            barrier,
+            inc=1,
+            device_id={"zon": pz, "mer": pm},
+            device_id_type=pl.DeviceIdType.MESH,
+        )
+        return carry
+
+    lax.fori_loop(0, count - 1, greet, 0)
+    pl.semaphore_wait(barrier, count - 1)
+
+    def launch(k, carry):
+        out_copy(k).start()
+        return carry
+
+    lax.fori_loop(0, count - 1, launch, 0)
+
+    prepare_kernel(sea_ref, forcing_ref, weights_ref, excess_ref, mask_ref, body_ref, edge)
+
+    def ice(at, from_ref):
+        current = (from_ref[at, 0], from_ref[at, 1])
+        east, north = ice_block(
+            mass_ref[at],
+            coriolis_ref[at],
+            (start_ref[0, at], start_ref[1, at]),
+            (wind_ref[0, at], wind_ref[1, at]),
+            current,
+        )
+        velocity_ref[0, at] = east
+        velocity_ref[1, at] = north
+        return drag_coeff * (east - current[0]), drag_coeff * (north - current[1])
+
+    own_east, own_north = ice(me, values_ref)
+    returned_ref[me, 0] = own_east
+    returned_ref[me, 1] = own_north
+
+    rim = around(
+        sizes, body_ref, edge, east_ref, west_ref, south_ref, north_ref, send_rim, recv_rim
+    )
+    for copy in rim:
+        copy.start()
+
+    def step(k, carry):
+        out_copy(k).wait_recv()
+        pz, pm = behind(k)
+        east, north = ice(pz * nm + pm, arrived)
+        drag[k, 0] = east
+        drag[k, 1] = north
+
+        @pl.when(k > 0)
+        def _():
+            back_copy(k - 1).start()
+
+        return carry
+
+    lax.fori_loop(0, count - 1, step, 0)
+    inverse_kernel(cols_ref, inverse_ref, count - 2, back_copy)
+
+    def finish(k, carry):
+        out_copy(k).wait_send()
+        back_copy(k).wait()
+        return carry
+
+    lax.fori_loop(0, count - 1, finish, 0)
+    for copy in rim:
+        copy.wait()
 
 
 def scatter_kernel(pairs, drag_ref, blocks_ref, inverse_ref, out_ref, edge_ref, total):
@@ -198,11 +342,45 @@
     pack_edges([out_ref.at[k] for k in range(out_ref.shape[0])], edge_ref)
 
 
-def widen_kernel(body_ref, east_ref, west_ref, tile_ref, rows_ref):
+def sweep_kernel(
+    sizes,
+    stress_ref, stress_edge_ref, body_ref, east_ref, west_ref, south_ref, north_ref,
+    out_ref,
+    field, wide_ref, even_ref, odd_ref, late_east, late_west, late_south, late_north, send, recv,
+):
     arrays, rows, width = body_ref.shape
+    tall, wide = rows + 2 * ROW_RIM, width + LANES
+    half = tall // 2
+    tiles = wide // LANES
     per = LANES // COL_RIM
-    slot = lax.broadcasted_iota(jnp.int32, (rows, LANES), 1) // COL_RIM
-    for k in range(arrays):
+    nz, nm = sizes
+    z, m = lax.axis_index("zon"), lax.axis_index("mer")
+    barrier = pltpu.get_barrier_semaphore()
+    for dz in (-1, 0, 1):
+        for dm in (-1, 0, 1):
+            if dz or dm:
+                pl.semaphore_signal(
+                    barrier,
+                    inc=1,
+                    device_id={"zon": lax.rem(z + dz + nz, nz), "mer": lax.rem(m + dm + nm, nm)},
+                    device_id_type=pl.DeviceIdType.MESH,
+                )
+    pl.semaphore_wait(barrier, 8)
+    rim = around(
+        sizes, stress_ref, stress_edge_ref, late_east, late_west, late_south, late_north, send, recv
+    )
+    for copy in rim:
+        copy.start()
+
+    row = lax.broadcasted_iota(jnp.int32, (tall, LANES), 0)
+    slot = lax.broadcasted_iota(jnp.int32, (tall, LANES), 1) // COL_RIM
+    lower = jnp.where(m == nm - 1, rows, rows + ROW_RIM)
+    upper = jnp.where(m == 0, tall, rows + ROW_RIM)
+    known = (row < lower) | ((row >= rows + ROW_RIM) & (row >= upper))
+    has_south = m < nm - 1
+    has_north = m > 0
+
+    def side_tile(k, east_ref, west_ref):
         at = (k // per) * LANES
         spot = k % per
         east = east_ref[:, at : at + LANES]
@@ -211,40 +389,25 @@
             east = pltpu.roll(east, LANES - spot * COL_RIM, 1)
         if spot != per - 1:
             west = pltpu.roll(west, LANES - (spot + 1) * COL_RIM, 1)
-        tile_ref[k] = jnp.where(slot == 0, east, jnp.where(slot == per - 1, west, 0.0))
-        for side, start in ((0, 0), (1, rows - ROW_RIM)):
-            rows_ref[side, k, :, :width] = body_ref[k, start : start + ROW_RIM, :]
-            rows_ref[side, k, :, width:] = tile_ref[k, start : start + ROW_RIM, :]
-
-
-def sweep_kernel(
-    body_ref, tile_ref, south_ref, north_ref,
-    stress_ref, stress_tile_ref, stress_south_ref, stress_north_ref,
-    out_ref, field, wide_ref, even_ref, odd_ref,
-):
-    arrays, rows, width = body_ref.shape
-    tall, wide = rows + 2 * ROW_RIM, width + LANES
-    half = tall // 2
-    tiles = wide // LANES
-
-    def gather_into(k, body, tile, south, north):
-        for t in range(tiles):
+        both = jnp.where(slot == 0, east, jnp.where(slot == per - 1, west, 0.0))
+        return jnp.where(known, both, 0.0)
+
+    for k in range(arrays):
+        for t in range(tiles - 1):
             at = k * tiles + t
             part = slice(t * LANES, (t + 1) * LANES)
-            field[at, :rows, :] = body[:, part] if t < tiles - 1 else tile[...]
-            field[at, rows : rows + ROW_RIM, :] = south[:, part]
-            field[at, rows + ROW_RIM :, :] = north[:, part]
-
-    for k in range(arrays):
-        gather_into(k, body_ref.at[k], tile_ref.at[k], south_ref.at[k], north_ref.at[k])
+            field[at, :rows, :] = body_ref[k, :, part]
+            field[at, rows : rows + ROW_RIM, :] = jnp.where(has_south, south_ref[k, :, part], 0.0)
+            field[at, rows + ROW_RIM :, :] = jnp.where(has_north, north_ref[k, :, part], 0.0)
+        field[k * tiles + tiles - 1] = side_tile(k, east_ref, west_ref)
     for c in range(2):
-        for ref, start, size, left, length in (
-            (stress_ref, 0, rows, 0, width),
-            (stress_tile_ref, 0, rows, width, LANES),
-            (stress_south_ref, rows, ROW_RIM, 0, wide),
-            (stress_north_ref, rows + ROW_RIM, ROW_RIM, 0, wide),
-        ):
-            wide_ref[c, start : start + size, left : left + length] = ref[c]
+        wide_ref[c, :rows, :width] = stress_ref[c]
+    for copy in rim:
+        copy.wait()
+    for c in range(2):
+        wide_ref[c, rows : rows + ROW_RIM, :width] = jnp.where(has_south, late_south[c], 0.0)
+        wide_ref[c, rows + ROW_RIM :, :width] = jnp.where(has_north, late_north[c], 0.0)
+        wide_ref[c, :, width:] = side_tile(c, late_east, late_west)
     east_stress = wide_ref[0]
     north_stress = wide_ref[1]
     change = (
@@ -299,33 +462,6 @@
         field[t, pl.ds(0, rows // 2, stride=2), :] = even_ref[: rows // 2, part]
         field[t, pl.ds(1, rows // 2, stride=2), :] = odd_ref[: rows // 2, part]
         out_ref[:, part] = field[t, :rows, :]
-
-
-def shift(values, axis, step, wrap):
-    count = lax.axis_size(axis)
-    pairs = [(i, (i + step) % count) for i in range(count) if wrap or 0 <= i + step < count]
-    return lax.ppermute(values, axis, pairs)
-
-
-def widen(body, edge):
-    arrays, rows, width = body.shape
-    east = shift(edge[0], "zon", -1, True)
-    west = shift(edge[1], "zon", 1, True)
-    tile, ends = pl.pallas_call(
-        widen_kernel,
-        out_shape=(
-            jax.ShapeDtypeStruct((arrays, rows, LANES), jnp.float32),
-            jax.ShapeDtypeStruct((2, arrays, ROW_RIM, width + LANES), jnp.float32),
-        ),
-        in_specs=[VM] * 3,
-        out_specs=(VM, VM),
-        compiler_params=PARAMS,
-        cost_estimate=cost(arrays * rows * 1024, arrays * rows * 1024),
-        name="widen",
-    )(body, east, west)
-    south = shift(ends[0], "mer", -1, False)
-    north = shift(ends[1], "mer", 1, False)
-    return tile, south, north
 
 
 def local(
@@ -347,7 +483,6 @@
     slots = devices * pairs
     tiles = width // LANES
     f32 = jnp.float32
-    names = ("zon", "mer")
     blocks = block_rows(intersection_block.reshape(slots // LANES, LANES), tiles, rows)
     cols = intersection_cols.reshape(slots, block)
     ice_shape = (devices, pairs, block)
@@ -363,58 +498,54 @@
         cost_estimate=cost(slots * rows * tiles * 1536, 4 * slot_bytes),
         name="pick",
     )(current, blocks, cols)
-    ice_current = lax.all_to_all(values, names, split_axis=0, concat_axis=0, tiled=True)
-
-    inverse = pl.pallas_call(
-        inverse_kernel,
-        out_shape=jax.ShapeDtypeStruct((slots, block), jnp.int32),
-        in_specs=[VM],
-        out_specs=VM,
-        compiler_params=PARAMS,
-        cost_estimate=cost(slots * block * 4096, 4 * slot_bytes),
-        name="inverse",
-    )(cols)
+    sizes = (lax.axis_size("zon"), lax.axis_size("mer"))
     arrays = 11
+    tall, wide = rows + 2 * ROW_RIM, width + LANES
     edge_width = -(-arrays * COL_RIM // LANES) * LANES
-    body, edge = pl.pallas_call(
-        prepare_kernel,
-        out_shape=(
-            jax.ShapeDtypeStruct((arrays, rows, width), f32),
-            jax.ShapeDtypeStruct((2, rows, edge_width), f32),
-        ),
-        in_specs=[VM] * 5,
-        out_specs=(VM, VM),
-        compiler_params=PARAMS,
-        cost_estimate=cost(rows * width * 64, rows * width * 96),
-        name="prepare",
-    )(sea_level, forcing, link_weights, excess, ocean_mask)
-    tile, south, north = widen(body, edge)
-
-    steps = 4
-    part = devices // steps
-    one = pl.BlockSpec((part, pairs, block), lambda i: (i, 0, 0))
-    two = pl.BlockSpec((2, part, pairs, block), lambda i: (0, i, 0, 0))
-    turned = pl.BlockSpec((part, 2, pairs, block), lambda i: (i, 0, 0, 0))
-    velocity, drag = pl.pallas_call(
-        ice_kernel,
-        grid=(steps,),
+    dma = pltpu.SemaphoreType.DMA
+    velocity, returned, inverse, body, east, west, south, north = pl.pallas_call(
+        functools.partial(travel_kernel, sizes),
         out_shape=(
             jax.ShapeDtypeStruct((2,) + ice_shape, f32),
             jax.ShapeDtypeStruct((devices, 2, pairs, block), f32),
+            jax.ShapeDtypeStruct((slots, block), jnp.int32),
+            jax.ShapeDtypeStruct((arrays, rows, width), f32),
+            jax.ShapeDtypeStruct((tall, edge_width), f32),
+            jax.ShapeDtypeStruct((tall, edge_width), f32),
+            jax.ShapeDtypeStruct((arrays, ROW_RIM, width), f32),
+            jax.ShapeDtypeStruct((arrays, ROW_RIM, width), f32),
         ),
-        in_specs=[one, one, two, two, turned],
-        out_specs=(two, turned),
-        compiler_params=PARAMS,
-        cost_estimate=cost(slots * block * 80, 12 * slot_bytes),
-        name="ice",
+        in_specs=[VM] * 11,
+        out_specs=(VM,) * 8,
+        scratch_shapes=[
+            pltpu.VMEM((devices, 2, pairs, block), f32),
+            pltpu.VMEM((devices, 2, pairs, block), f32),
+            pltpu.VMEM((2, rows, edge_width), f32),
+            dma((devices,)),
+            dma((devices,)),
+            dma((devices,)),
+            dma((devices,)),
+            dma((8,)),
+            dma((8,)),
+        ],
+        compiler_params=pltpu.CompilerParams(
+            vmem_limit_bytes=48 * 1024 * 1024, collective_id=0, has_side_effects=True
+        ),
+        cost_estimate=cost(slots * block * 4096, 16 * slot_bytes),
+        name="travel",
     )(
+        values,
         ice_mass.reshape(ice_shape),
         coriolis.reshape(ice_shape),
         ice_start.reshape((2,) + ice_shape),
         wind_stress.reshape((2,) + ice_shape),
-        ice_current,
+        sea_level,
+        forcing,
+        link_weights,
+        excess,
+        ocean_mask,
+        cols,
     )
-    returned = lax.all_to_all(drag, names, split_axis=0, concat_axis=0, tiled=True)
 
     stress, stress_edge = pl.pallas_call(
         functools.partial(scatter_kernel, pairs),
@@ -429,24 +560,29 @@
         cost_estimate=cost(slots * rows * tiles * 1536, 4 * slot_bytes),
         name="put",
     )(returned, blocks, inverse)
-    stress_tile, stress_south, stress_north = widen(stress, stress_edge)
-
-    tall, wide = rows + 2 * ROW_RIM, width + LANES
     surface = pl.pallas_call(
-        sweep_kernel,
+        functools.partial(sweep_kernel, sizes),
         out_shape=jax.ShapeDtypeStruct((rows, width), f32),
-        in_specs=[VM] * 8,
+        in_specs=[VM] * 7,
         out_specs=VM,
         scratch_shapes=[
             pltpu.VMEM((arrays * (wide // LANES), tall, LANES), f32),
             pltpu.VMEM((2, tall, wide), f32),
             pltpu.VMEM((tall // 2, wide), f32),
             pltpu.VMEM((tall // 2, wide), f32),
+            pltpu.VMEM((tall, LANES), f32),
+            pltpu.VMEM((tall, LANES), f32),
+            pltpu.VMEM((2, ROW_RIM, width), f32),
+            pltpu.VMEM((2, ROW_RIM, width), f32),
+            dma((8,)),
+            dma((8,)),
         ],
-        compiler_params=PARAMS,
+        compiler_params=pltpu.CompilerParams(
+            vmem_limit_bytes=48 * 1024 * 1024, collective_id=1, has_side_effects=True
+        ),
         cost_estimate=cost(rows * width * 200, rows * width * 64),
         name="sweep",
-    )(body, tile, south, north, stress, stress_tile, stress_south, stress_north)
+    )(stress, stress_edge, body, east, west, south, north)
     return (surface, velocity.reshape((2, 1) + ice_shape))
 
 

time: 105 us -> 102 us (0.971)
  the two profiles are of different devices: /device:TPU:1 before, /device:TPU:17 now
where the time goes in v2:
time: 102 us
  Pallas kernels  94.2 us (92%)
  local copies, waits for them, and re-layouts  5.08 us (5%)
  other arithmetic  1.47 us (1%)
    pallas_call x1, Pallas kernels, local(): pl.pallas_call(functools.partial(travel_kernel, sizes), out_shape=(jax.Sh...  80 us
    pallas_call x1, Pallas kernels, local(): pl.pallas_call(functools.partial(sweep_kernel, sizes), out_shape=jax.Shap...  10.8 us
    unnamed x24, local copies, waits for them, and re-layouts  4.76 us
    pallas_call x1, Pallas kernels, local(): pl.pallas_call(functools.partial(scatter_kernel, pairs), out_shape=(jax.S...  2.09 us

profile of v2, /device:TPU:17, one launch (start us, length us, event | category | flops | bytes accessed | tf_op | source)
XLA Modules:
  0.0 101.5 jit_solution(14699954696983182688)
XLA Ops:
  0.6 0.7 sign_compare_fusion
  1.4 0.1 ne.26
  1.4 0.1 ge.7
  1.5 0.7 maximum_shift-right-logical_fusion
  2.3 0.1 div.12
  2.3 0.1 rem.18
  2.4 0.0 copy-start.2
  2.4 1.0 %copy-done.2 = s32[1,32,32,128]{3,2,1,0:T(8,128)S(1)} copy-done((s32[1,32,32,128]{3,2,1,0:T(8,128)S(1)}, s32[1,32,32,128]{3,2,1,0:T(8,128)}, u32[]{:S(2)}) %copy-start.2) | copy-done | bytes 524312
  3.5 0.0 copy-start.10
  3.5 1.0 %copy-done.10 = f32[2,128,512]{2,1,0:T(8,128)S(1)} copy-done((f32[2,128,512]{2,1,0:T(8,128)S(1)}, f32[2,128,512]{2,1,0:T(8,128)}, u32[]{:S(2)}) %copy-start.10) | copy-done | bytes 524312
  4.5 0.0 copy-start.3
  4.5 0.0 copy-start.4
  4.5 0.0 copy-start.5
  4.5 0.0 copy-start.6
  4.5 0.0 copy-start.7
  4.5 0.0 copy-start.8
  4.5 0.0 copy-start.9
  4.6 1.3 %pick.1.values_ref = f32[32,2,32,128]{3,2,1,0:T(8,128)S(1)} custom-call(f32[2,128,512]{2,1,0:T(8,128)S(1)} %copy-done.10, s32[8,128]{1,0:T(8,128)S(1)} %fusion.2.blocks_ref, s32[1024,128]{1,0:T(8,128)S(1)} %bitcast.9), custom_call_target="tpu_custom_call" | custom-call | flops 805306368 | bytes 2097152 | tf_op jit(solution)/shard_map/pick/pallas_call | solution.py:491
  5.8 0.0 copy-start.1
  5.8 1.0 copy-done.1
  6.8 0.0 copy-done.3
  6.8 0.0 copy-done.4
  6.8 0.0 copy-done.5
  6.8 0.0 copy-done.6
  6.8 0.0 copy-done.7
  6.8 0.0 copy-done.8
  6.9 0.0 copy-done.9
  6.9 80.0 %travel.1 = (f32[2,32,32,128]{3,2,1,0:T(8,128)S(1)}, f32[32,2,32,128]{3,2,1,0:T(8,128)S(1)}, s32[1024,128]{1,0:T(8,128)S(1)}, f32[11,128,512]{2,1,0:T(8,128)}, f...) custom-call(f32[32,2,32,128]{3,2,1,0:T(8,128)} %copy-done.1, ...), custom_call_target="tpu_custom_call" | custom-call | flops 536870912 | bytes 8388608 | tf_op jit(solution)/shard_map/travel/pallas_call | solution.py:506
  86.9 0.0 copy-start
  86.9 2.1 %put.1 = (f32[2,128,512]{2,1,0:T(8,128)S(1)}, f32[2,128,128]{2,1,0:T(8,128)S(1)}) custom-call(f32[32,2,32,128]{3,2,1,0:T(8,128)S(1)} %get-tuple-element.12.drag_ref, s32[8,128]{1,0:T(8,128)S(1)} %fusion.2.blocks_ref, s32[1024,128]{1,0:T(8,128)S(1)} %get-tuple-element.13.inverse_ref), custom_call_target="tpu_custom_call" | custom-call | flops 805306368 | bytes 2097152 | tf_op jit(solution)/shard_map/put/pallas_call | solution.py:550
  89.0 0.0 copy-done
  89.0 10.8 %sweep.1 = f32[128,512]{1,0:T(8,128)S(1)} custom-call(f32[2,128,512]{2,1,0:T(8,128)S(1)} %get-tuple-element.14.stress_ref, f32[2,128,128]{2,1,0:T(8,128)S(1)} %get-tuple-element.15.stress_edge_ref, f32[11,128,512]{2,1,0:T(8,128)S(1)} %copy-done, f32[144,256]{1,0:T(8,128)S(1)} %get-tuple-element.17.east_ref, f32[144,256]{1,0:T(8,128)S(1)} %get-tuple-element.18.west_ref, ...), custom_call_target="tpu_custom_call" | custom-call | flops 13107200 | bytes 4194304 | tf_op jit(solution)/shard_map/sweep/pallas_call | solution.py:563
  99.9 0.7 copy.17
  100.6 1.0 copy.18
  (1 shorter events, 0.0 us)
Async XLA Ops:
  2.4 1.0 %copy-start.2 = (s32[1,32,32,128]{3,2,1,0:T(8,128)S(1)}, s32[1,32,32,128]{3,2,1,0:T(8,128)}, u32[]{:S(2)}) copy-start(s32[1,32,32,128]{3,2,1,0:T(8,128)} %param.19) | copy-start | bytes 1572868
  3.5 1.0 %copy-start.10 = (f32[2,128,512]{2,1,0:T(8,128)S(1)}, f32[2,128,512]{2,1,0:T(8,128)}, u32[]{:S(2)}) copy-start(f32[2,128,512]{2,1,0:T(8,128)} %current_ref.1) | copy-start | bytes 1572868
  4.5 2.3 %copy-start.3 = (s32[1,32,32,128]{3,2,1,0:T(8,128)S(1)}, s32[1,32,32,128]{3,2,1,0:T(8,128)}, u32[]{:S(2)}) copy-start(s32[1,32,32,128]{3,2,1,0:T(8,128)} %param.19) | copy-start | bytes 1572868
  4.5 2.3 %copy-start.4 = (f32[1,32,32,128]{3,2,1,0:T(8,128)S(1)}, f32[1,32,32,128]{3,2,1,0:T(8,128)}, u32[]{:S(2)}) copy-start(f32[1,32,32,128]{3,2,1,0:T(8,128)} %param.20) | copy-start | bytes 1572868
  4.5 2.3 %copy-start.5 = (f32[1,32,32,128]{3,2,1,0:T(8,128)S(1)}, f32[1,32,32,128]{3,2,1,0:T(8,128)}, u32[]{:S(2)}) copy-start(f32[1,32,32,128]{3,2,1,0:T(8,128)} %param.21) | copy-start | bytes 1572868
  4.5 2.3 %copy-start.6 = (f32[128,512]{1,0:T(8,128)S(1)}, f32[128,512]{1,0:T(8,128)}, u32[]{:S(2)}) copy-start(f32[128,512]{1,0:T(8,128)} %sea_ref.1) | copy-start | bytes 786436
  4.5 2.3 %copy-start.7 = (f32[128,512]{1,0:T(8,128)S(1)}, f32[128,512]{1,0:T(8,128)}, u32[]{:S(2)}) copy-start(f32[128,512]{1,0:T(8,128)} %forcing_ref.1) | copy-start | bytes 786436
  4.5 2.3 %copy-start.8 = (f32[128,512]{1,0:T(8,128)S(1)}, f32[128,512]{1,0:T(8,128)}, u32[]{:S(2)}) copy-start(f32[128,512]{1,0:T(8,128)} %excess_ref.1) | copy-start | bytes 786436
  4.5 2.3 %copy-start.9 = (s32[128,512]{1,0:T(8,128)S(1)}, s32[128,512]{1,0:T(8,128)}, u32[]{:S(2)}) copy-start(s32[128,512]{1,0:T(8,128)} %mask_ref.1) | copy-start | bytes 786436
  5.8 1.0 copy-start.1
  86.9 2.1 %copy-start = (f32[11,128,512]{2,1,0:T(8,128)S(1)}, f32[11,128,512]{2,1,0:T(8,128)}, u32[]{:S(2)}) copy-start(f32[11,128,512]{2,1,0:T(8,128)} %get-tuple-element.16.body_ref) | copy-start | bytes 8650756

commit v3 on v2

--- a/solution.py
+++ b/solution.py
@@ -72,35 +72,26 @@
                 out_ref[g * (LANES // pairs) + d, c] = taken[d * pairs : (d + 1) * pairs]
 
 
-def inverse_kernel(cols_ref, out_ref, last, back_copy):
+def inverse_rows(cols):
     lane = lax.broadcasted_iota(jnp.int32, (8, LANES), 1)
     sub = lax.broadcasted_iota(jnp.int32, (8, LANES), 0)
     order = (lane + 1).astype(jnp.float32)
     index = (lane % 16) * 8 + sub
     group = lane // 16
-
-    def body(i, carry):
-        at = pl.multiple_of(i * 8, 8)
-        cols = cols_ref[pl.ds(at, 8), :]
-        high = jnp.right_shift(cols, 4)
-        low = jnp.bitwise_and(cols, 15)
-        left = jnp.concatenate([jnp.where(high == h, 1.0, 0.0) for h in range(8)], axis=0)
-        right = jnp.concatenate([jnp.where(low == b, order, 0.0) for b in range(16)], axis=0)
-        product = lax.dot_general(
-            left.astype(jnp.bfloat16),
-            right.astype(jnp.bfloat16),
-            (((1,), (1,)), ((), ())),
-            preferred_element_type=jnp.float32,
-        )
-        found = jnp.zeros((8, LANES), jnp.float32)
-        for h in range(8):
-            found = jnp.where(group == h, lane_take(product[h * 8 : (h + 1) * 8], index), found)
-        out_ref[pl.ds(at, 8), :] = found.astype(jnp.int32) - 1
-        return carry
-
-    lax.fori_loop(0, 1, body, 0)
-    back_copy(last).start()
-    lax.fori_loop(1, cols_ref.shape[0] // 8, body, 0)
+    high = jnp.right_shift(cols, 4)
+    low = jnp.bitwise_and(cols, 15)
+    left = jnp.concatenate([jnp.where(high == h, 1.0, 0.0) for h in range(8)], axis=0)
+    right = jnp.concatenate([jnp.where(low == b, order, 0.0) for b in range(16)], axis=0)
+    product = lax.dot_general(
+        left.astype(jnp.bfloat16),
+        right.astype(jnp.bfloat16),
+        (((1,), (1,)), ((), ())),
+        preferred_element_type=jnp.float32,
+    )
+    found = jnp.zeros((8, LANES), jnp.float32)
+    for h in range(8):
+        found = jnp.where(group == h, lane_take(product[h * 8 : (h + 1) * 8], index), found)
+    return found.astype(jnp.int32) - 1
 
 
 def ice_block(mass, coriolis, start, wind, current):
@@ -240,7 +231,14 @@
         velocity_ref[1, at] = north
         return drag_coeff * (east - current[0]), drag_coeff * (north - current[1])
 
+    pairs = mass_ref.shape[1]
+
+    def invert(k):
+        for r in range(0, pairs, 8):
+            inverse_ref[k, r : r + 8] = inverse_rows(cols_ref[k, r : r + 8])
+
     own_east, own_north = ice(me, values_ref)
+    invert(count - 1)
     returned_ref[me, 0] = own_east
     returned_ref[me, 1] = own_north
 
@@ -256,6 +254,7 @@
         east, north = ice(pz * nm + pm, arrived)
         drag[k, 0] = east
         drag[k, 1] = north
+        invert(k)
 
         @pl.when(k > 0)
         def _():
@@ -264,7 +263,7 @@
         return carry
 
     lax.fori_loop(0, count - 1, step, 0)
-    inverse_kernel(cols_ref, inverse_ref, count - 2, back_copy)
+    back_copy(count - 2).start()
 
     def finish(k, carry):
         out_copy(k).wait_send()
@@ -508,7 +507,7 @@
         out_shape=(
             jax.ShapeDtypeStruct((2,) + ice_shape, f32),
             jax.ShapeDtypeStruct((devices, 2, pairs, block), f32),
-            jax.ShapeDtypeStruct((slots, block), jnp.int32),
+            jax.ShapeDtypeStruct((devices, pairs, block), jnp.int32),
             jax.ShapeDtypeStruct((arrays, rows, width), f32),
             jax.ShapeDtypeStruct((tall, edge_width), f32),
             jax.ShapeDtypeStruct((tall, edge_width), f32),
@@ -544,7 +543,7 @@
         link_weights,
         excess,
         ocean_mask,
-        cols,
+        intersection_cols[0],
     )
 
     stress, stress_edge = pl.pallas_call(
@@ -559,7 +558,7 @@
         compiler_params=PARAMS,
         cost_estimate=cost(slots * rows * tiles * 1536, 4 * slot_bytes),
         name="put",
-    )(returned, blocks, inverse)
+    )(returned, blocks, inverse.reshape(slots, block))
     surface = pl.pallas_call(
         functools.partial(sweep_kernel, sizes),
         out_shape=jax.ShapeDtypeStruct((rows, width), f32),

time: 102 us -> 83.2 us (0.82)
  the two profiles are of different devices: /device:TPU:17 before, /device:TPU:1 now
where the time goes in v3:
time: 83.2 us; the launch traced here: 82.5 us
  Pallas kernels  75.2 us (90%)
  local copies, waits for them, and re-layouts  5.08 us (6%)
  other arithmetic  1.47 us (2%)
    pallas_call x1, Pallas kernels, local(): pl.pallas_call(functools.partial(travel_kernel, sizes), out_shape=(jax.Sh...  59.4 us
    pallas_call x1, Pallas kernels, local(): pl.pallas_call(functools.partial(sweep_kernel, sizes), out_shape=jax.Shap...  12.4 us
    unnamed x24, local copies, waits for them, and re-layouts  4.76 us
    pallas_call x1, Pallas kernels, local(): pl.pallas_call(functools.partial(scatter_kernel, pairs), out_shape=(jax.S...  2.08 us

profile of v3, /device:TPU:1, one launch (start us, length us, event | category | flops | bytes accessed | tf_op | source)
XLA Modules:
  0.0 82.5 jit_solution(4257221406187750214)
XLA Ops:
  0.6 0.7 sign_compare_fusion
  1.4 0.1 ne.26
  1.4 0.1 ge.7
  1.5 0.7 maximum_shift-right-logical_fusion
  2.3 0.1 div.12
  2.3 0.1 rem.18
  2.4 0.0 copy-start.2
  2.4 1.0 %copy-done.2 = s32[1,32,32,128]{3,2,1,0:T(8,128)S(1)} copy-done((s32[1,32,32,128]{3,2,1,0:T(8,128)S(1)}, s32[1,32,32,128]{3,2,1,0:T(8,128)}, u32[]{:S(2)}) %copy-start.2) | copy-done | bytes 524312
  3.5 0.0 copy-start.10
  3.5 1.0 %copy-done.10 = f32[2,128,512]{2,1,0:T(8,128)S(1)} copy-done((f32[2,128,512]{2,1,0:T(8,128)S(1)}, f32[2,128,512]{2,1,0:T(8,128)}, u32[]{:S(2)}) %copy-start.10) | copy-done | bytes 524312
  4.5 0.0 copy-start.3
  4.5 0.0 copy-start.4
  4.5 0.0 copy-start.5
  4.5 0.0 copy-start.6
  4.5 0.0 copy-start.7
  4.5 0.0 copy-start.8
  4.5 0.0 copy-start.9
  4.6 1.3 %pick.1.values_ref = f32[32,2,32,128]{3,2,1,0:T(8,128)S(1)} custom-call(f32[2,128,512]{2,1,0:T(8,128)S(1)} %copy-done.10, s32[8,128]{1,0:T(8,128)S(1)} %fusion.2.blocks_ref, s32[1024,128]{1,0:T(8,128)S(1)} %bitcast.11), custom_call_target="tpu_custom_call" | custom-call | flops 805306368 | bytes 2097152 | tf_op jit(solution)/shard_map/pick/pallas_call | solution.py:490
  5.8 0.0 copy-start.1
  5.8 1.0 %copy-done.1 = f32[32,2,32,128]{3,2,1,0:T(8,128)} copy-done((f32[32,2,32,128]{3,2,1,0:T(8,128)}, f32[32,2,32,128]{3,2,1,0:T(8,128)S(1)}, u32[]{:S(2)}) %copy-start.1) | copy-done | bytes 1048600
  6.8 0.0 copy-done.3
  6.8 0.0 copy-done.4
  6.8 0.0 copy-done.5
  6.8 0.0 copy-done.6
  6.8 0.0 copy-done.7
  6.8 0.0 copy-done.8
  6.9 0.0 copy-done.9
  6.9 59.4 %travel.1 = (f32[2,32,32,128]{3,2,1,0:T(8,128)S(1)}, f32[32,2,32,128]{3,2,1,0:T(8,128)S(1)}, s32[32,32,128]{2,1,0:T(8,128)S(1)}, f32[11,128,512]{2,1,0:T(8,128)}...) custom-call(f32[32,2,32,128]{3,2,1,0:T(8,128)} %copy-done.1, ...), custom_call_target="tpu_custom_call" | custom-call | flops 536870912 | bytes 8388608 | tf_op jit(solution)/shard_map/travel/pallas_call | solution.py:505
  66.2 0.0 copy-start
  66.2 2.1 %put.1 = (f32[2,128,512]{2,1,0:T(8,128)S(1)}, f32[2,128,128]{2,1,0:T(8,128)S(1)}) custom-call(f32[32,2,32,128]{3,2,1,0:T(8,128)S(1)} %get-tuple-element.12.drag_ref, s32[8,128]{1,0:T(8,128)S(1)} %fusion.2.blocks_ref, s32[1024,128]{1,0:T(8,128)S(1)} %bitcast.15), custom_call_target="tpu_custom_call" | custom-call | flops 805306368 | bytes 2097152 | tf_op jit(solution)/shard_map/put/pallas_call | solution.py:549
  68.3 0.0 copy-done
  68.3 12.4 %sweep.1 = f32[128,512]{1,0:T(8,128)S(1)} custom-call(f32[2,128,512]{2,1,0:T(8,128)S(1)} %get-tuple-element.14.stress_ref, f32[2,128,128]{2,1,0:T(8,128)S(1)} %get-tuple-element.15.stress_edge_ref, f32[11,128,512]{2,1,0:T(8,128)S(1)} %copy-done, f32[144,256]{1,0:T(8,128)S(1)} %get-tuple-element.17.east_ref, f32[144,256]{1,0:T(8,128)S(1)} %get-tuple-element.18.west_ref, ...), custom_call_target="tpu_custom_call" | custom-call | flops 13107200 | bytes 4194304 | tf_op jit(solution)/shard_map/sweep/pallas_call | solution.py:562
  80.8 0.7 copy.17
  81.5 1.0 %copy.18 = f32[2,1,32,32,128]{4,3,2,1,0:T(8,128)} copy(f32[2,1,32,32,128]{4,3,2,1,0:T(8,128)S(1)} %bitcast.10) | data formatting | bytes 2097152
  (1 shorter events, 0.0 us)
Async XLA Ops:
  2.4 1.0 %copy-start.2 = (s32[1,32,32,128]{3,2,1,0:T(8,128)S(1)}, s32[1,32,32,128]{3,2,1,0:T(8,128)}, u32[]{:S(2)}) copy-start(s32[1,32,32,128]{3,2,1,0:T(8,128)} %param.19) | copy-start | bytes 1572868
  3.5 1.0 %copy-start.10 = (f32[2,128,512]{2,1,0:T(8,128)S(1)}, f32[2,128,512]{2,1,0:T(8,128)}, u32[]{:S(2)}) copy-start(f32[2,128,512]{2,1,0:T(8,128)} %current_ref.1) | copy-start | bytes 1572868
  4.5 2.3 %copy-start.3 = (s32[1,32,32,128]{3,2,1,0:T(8,128)S(1)}, s32[1,32,32,128]{3,2,1,0:T(8,128)}, u32[]{:S(2)}) copy-start(s32[1,32,32,128]{3,2,1,0:T(8,128)} %param.19) | copy-start | bytes 1572868
  4.5 2.3 %copy-start.4 = (f32[1,32,32,128]{3,2,1,0:T(8,128)S(1)}, f32[1,32,32,128]{3,2,1,0:T(8,128)}, u32[]{:S(2)}) copy-start(f32[1,32,32,128]{3,2,1,0:T(8,128)} %param.20) | copy-start | bytes 1572868
  4.5 2.3 %copy-start.5 = (f32[1,32,32,128]{3,2,1,0:T(8,128)S(1)}, f32[1,32,32,128]{3,2,1,0:T(8,128)}, u32[]{:S(2)}) copy-start(f32[1,32,32,128]{3,2,1,0:T(8,128)} %param.21) | copy-start | bytes 1572868
  4.5 2.3 %copy-start.6 = (f32[128,512]{1,0:T(8,128)S(1)}, f32[128,512]{1,0:T(8,128)}, u32[]{:S(2)}) copy-start(f32[128,512]{1,0:T(8,128)} %sea_ref.1) | copy-start | bytes 786436
  4.5 2.3 %copy-start.7 = (f32[128,512]{1,0:T(8,128)S(1)}, f32[128,512]{1,0:T(8,128)}, u32[]{:S(2)}) copy-start(f32[128,512]{1,0:T(8,128)} %forcing_ref.1) | copy-start | bytes 786436
  4.5 2.3 %copy-start.8 = (f32[128,512]{1,0:T(8,128)S(1)}, f32[128,512]{1,0:T(8,128)}, u32[]{:S(2)}) copy-start(f32[128,512]{1,0:T(8,128)} %excess_ref.1) | copy-start | bytes 786436
  4.5 2.3 %copy-start.9 = (s32[128,512]{1,0:T(8,128)S(1)}, s32[128,512]{1,0:T(8,128)}, u32[]{:S(2)}) copy-start(s32[128,512]{1,0:T(8,128)} %mask_ref.1) | copy-start | bytes 786436
  5.8 1.0 %copy-start.1 = (f32[32,2,32,128]{3,2,1,0:T(8,128)}, f32[32,2,32,128]{3,2,1,0:T(8,128)S(1)}, u32[]{:S(2)}) copy-start(f32[32,2,32,128]{3,2,1,0:T(8,128)S(1)} %pick.1.values_ref) | copy-start | bytes 3145732
  66.2 2.1 %copy-start = (f32[11,128,512]{2,1,0:T(8,128)S(1)}, f32[11,128,512]{2,1,0:T(8,128)}, u32[]{:S(2)}) copy-start(f32[11,128,512]{2,1,0:T(8,128)} %get-tuple-element.16.body_ref) | copy-start | bytes 8650756

commit v4 on v3

--- a/solution.py
+++ b/solution.py
@@ -16,6 +16,7 @@
 drag_coeff = 1.0
 link_coeff = 0.5
 VM = pl.BlockSpec(memory_space=pltpu.VMEM)
+HBM = pl.BlockSpec(memory_space=pltpu.HBM)
 PARAMS = pltpu.CompilerParams(vmem_limit_bytes=48 * 1024 * 1024)
 
 
@@ -44,16 +45,25 @@
     return jnp.where(blocks >= 0, (safe % tiles) * rows + safe // tiles, -1)
 
 
-def gather_kernel(pairs, current_ref, blocks_ref, cols_ref, out_ref, parts):
+def gather_kernel(
+    pairs, current_hbm, blocks_ref, cols_hbm, out_ref, parts, current_ref, cols_ref, loads
+):
     _, rows, width = current_ref.shape
     tiles = width // LANES
+    load_current = pltpu.make_async_copy(current_hbm, current_ref, loads.at[0])
+    load_cols = pltpu.make_async_copy(cols_hbm, cols_ref, loads.at[1])
+    load_current.start()
+    load_cols.start()
+    blocks = block_rows(blocks_ref[...], tiles, rows)
+    load_current.wait()
     for j in range(tiles):
         for c in range(2):
             for k, part in enumerate(split3(current_ref[c, :, j * LANES : (j + 1) * LANES])):
                 parts[k, j * rows : (j + 1) * rows, c * LANES : (c + 1) * LANES] = part
     lane = lax.broadcasted_iota(jnp.int32, (LANES, LANES), 1)
+    load_cols.wait()
     for g in range(blocks_ref.shape[0]):
-        spread = jnp.broadcast_to(blocks_ref[g : g + 1, :], (LANES, LANES))
+        spread = jnp.broadcast_to(blocks[g : g + 1, :], (LANES, LANES))
         turned = jnp.transpose(spread)
         pick = jnp.concatenate(
             [
@@ -275,14 +285,20 @@
         copy.wait()
 
 
-def scatter_kernel(pairs, drag_ref, blocks_ref, inverse_ref, out_ref, edge_ref, total):
+def scatter_kernel(
+    pairs, drag_ref, blocks_ref, inverse_ref, velocity_ref, out_ref, edge_ref, velocity_hbm,
+    total, write,
+):
     _, rows, width = out_ref.shape
     tiles = width // LANES
     count = rows * tiles
+    write_velocity = pltpu.make_async_copy(velocity_ref, velocity_hbm, write)
+    write_velocity.start()
+    blocks = block_rows(blocks_ref[...], tiles, rows)
     row = lax.broadcasted_iota(jnp.int32, (count, LANES), 0)
     for g in range(blocks_ref.shape[0]):
         put = jnp.where(
-            jnp.broadcast_to(blocks_ref[g : g + 1, :], (count, LANES)) == row, 1.0, 0.0
+            jnp.broadcast_to(blocks[g : g + 1, :], (count, LANES)) == row, 1.0, 0.0
         ).astype(jnp.bfloat16)
         inverse = inverse_ref[g * LANES : (g + 1) * LANES, :]
         index = jnp.maximum(inverse, 0)
@@ -304,6 +320,7 @@
                 j * rows : (j + 1) * rows, c * LANES : (c + 1) * LANES
             ]
     pack_edges([out_ref.at[0], out_ref.at[1]], edge_ref)
+    write_velocity.wait()
 
 
 def pack_edges(refs, edge_ref):
@@ -482,7 +499,7 @@
     slots = devices * pairs
     tiles = width // LANES
     f32 = jnp.float32
-    blocks = block_rows(intersection_block.reshape(slots // LANES, LANES), tiles, rows)
+    blocks = intersection_block.reshape(slots // LANES, LANES)
     cols = intersection_cols.reshape(slots, block)
     ice_shape = (devices, pairs, block)
     slot_bytes = slots * block * 4
@@ -490,9 +507,14 @@
     values = pl.pallas_call(
         functools.partial(gather_kernel, pairs),
         out_shape=jax.ShapeDtypeStruct((devices, 2, pairs, block), f32),
-        in_specs=[VM] * 3,
+        in_specs=[HBM, VM, HBM],
         out_specs=VM,
-        scratch_shapes=[pltpu.VMEM((3, rows * tiles, 2 * LANES), jnp.bfloat16)],
+        scratch_shapes=[
+            pltpu.VMEM((3, rows * tiles, 2 * LANES), jnp.bfloat16),
+            pltpu.VMEM((2, rows, width), f32),
+            pltpu.VMEM((slots, block), jnp.int32),
+            pltpu.SemaphoreType.DMA((2,)),
+        ],
         compiler_params=PARAMS,
         cost_estimate=cost(slots * rows * tiles * 1536, 4 * slot_bytes),
         name="pick",
@@ -546,19 +568,20 @@
         intersection_cols[0],
     )
 
-    stress, stress_edge = pl.pallas_call(
+    stress, stress_edge, velocity = pl.pallas_call(
         functools.partial(scatter_kernel, pairs),
         out_shape=(
             jax.ShapeDtypeStruct((2, rows, width), f32),
             jax.ShapeDtypeStruct((2, rows, LANES), f32),
+            jax.ShapeDtypeStruct((2,) + ice_shape, f32),
         ),
-        in_specs=[VM] * 3,
-        out_specs=(VM, VM),
-        scratch_shapes=[pltpu.VMEM((rows * tiles, 2 * LANES), f32)],
+        in_specs=[VM] * 4,
+        out_specs=(VM, VM, HBM),
+        scratch_shapes=[pltpu.VMEM((rows * tiles, 2 * LANES), f32), pltpu.SemaphoreType.DMA],
         compiler_params=PARAMS,
         cost_estimate=cost(slots * rows * tiles * 1536, 4 * slot_bytes),
         name="put",
-    )(returned, blocks, inverse.reshape(slots, block))
+    )(returned, blocks, inverse.reshape(slots, block), velocity)
     surface = pl.pallas_call(
         functools.partial(sweep_kernel, sizes),
         out_shape=jax.ShapeDtypeStruct((rows, width), f32),

time: 83.2 us -> 81.4 us (0.978)
  other arithmetic: 1.47 us -> 0 us
    unnamed x24 -> x23, local copies, waits for them, and re-layouts: 4.76 us -> 3.85 us
where the time goes in v4:
time: 81.4 us; the launch traced here: 80.7 us
  Pallas kernels  75.4 us (93%)
  local copies, waits for them, and re-layouts  4.64 us (6%)
    pallas_call x1, Pallas kernels, local(): pl.pallas_call(functools.partial(travel_kernel, sizes), out_shape=(jax.Sh...  59.3 us
    pallas_call x1, Pallas kernels, local(): pl.pallas_call(functools.partial(sweep_kernel, sizes), out_shape=jax.Shap...  12.4 us
    unnamed x23, local copies, waits for them, and re-layouts  3.85 us
    pallas_call x1, Pallas kernels, local(): pl.pallas_call(functools.partial(scatter_kernel, pairs), out_shape=(jax.S...  2.11 us

profile of v4, /device:TPU:1, one launch (start us, length us, event | category | flops | bytes accessed | tf_op | source)
XLA Modules:
  0.0 80.7 jit_solution(14930071842071813524)
XLA Ops:
  0.6 0.8 reshape.28.blocks_ref
  1.4 0.0 copy-start.2
  1.4 1.0 %copy-done.2 = s32[1,32,32,128]{3,2,1,0:T(8,128)S(1)} copy-done((s32[1,32,32,128]{3,2,1,0:T(8,128)S(1)}, s32[1,32,32,128]{3,2,1,0:T(8,128)}, u32[]{:S(2)}) %copy-start.2) | copy-done | bytes 524312
  2.5 0.0 copy-start.10
  2.5 1.0 %copy-done.10 = f32[2,128,512]{2,1,0:T(8,128)S(1)} copy-done((f32[2,128,512]{2,1,0:T(8,128)S(1)}, f32[2,128,512]{2,1,0:T(8,128)}, u32[]{:S(2)}) %copy-start.10) | copy-done | bytes 524312
  3.5 0.0 copy-start.3
  3.5 0.0 copy-start.4
  3.5 0.0 copy-start.5
  3.5 0.0 copy-start.6
  3.5 0.0 copy-start.7
  3.5 0.0 copy-start.8
  3.5 0.0 copy-start.9
  3.6 1.5 %pick.1.values_ref = f32[32,2,32,128]{3,2,1,0:T(8,128)S(1)} custom-call(f32[2,128,512]{2,1,0:T(8,128)S(1)} %copy-done.10, s32[8,128]{1,0:T(8,128)S(1)} %reshape.28.blocks_ref, s32[1024,128]{1,0:T(8,128)S(1)} %bitcast.10), custom_call_target="tpu_custom_call" | custom-call | flops 805306368 | bytes 2097152 | tf_op jit(solution)/shard_map/pick/pallas_call | solution.py:507
  5.0 0.0 copy-start.1
  5.1 1.0 %copy-done.1 = f32[32,2,32,128]{3,2,1,0:T(8,128)} copy-done((f32[32,2,32,128]{3,2,1,0:T(8,128)}, f32[32,2,32,128]{3,2,1,0:T(8,128)S(1)}, u32[]{:S(2)}) %copy-start.1) | copy-done | bytes 1048600
  6.0 0.0 copy-done.3
  6.0 0.0 copy-done.4
  6.0 0.0 copy-done.5
  6.0 0.0 copy-done.6
  6.0 0.0 copy-done.7
  6.0 0.0 copy-done.8
  6.0 0.0 copy-done.9
  6.1 59.3 %travel.1 = (f32[2,32,32,128]{3,2,1,0:T(8,128)S(1)}, f32[32,2,32,128]{3,2,1,0:T(8,128)S(1)}, s32[32,32,128]{2,1,0:T(8,128)S(1)}, f32[11,128,512]{2,1,0:T(8,128)}...) custom-call(f32[32,2,32,128]{3,2,1,0:T(8,128)} %copy-done.1, ...), custom_call_target="tpu_custom_call" | custom-call | flops 536870912 | bytes 8388608 | tf_op jit(solution)/shard_map/travel/pallas_call | solution.py:527
  65.4 0.0 copy-start
  65.4 2.1 %put.1 = (f32[2,128,512]{2,1,0:T(8,128)S(1)}, f32[2,128,128]{2,1,0:T(8,128)S(1)}, f32[2,32,32,128]{3,2,1,0:T(8,128)}) custom-call(f32[32,2,32,128]{3,2,1,0:T(8,128)S(1)} %get-tuple-element.13.drag_ref, s32[8,128]{1,0:T(8,128)S(1)} %reshape.28.blocks_ref, s32[1024,128]{1,0:T(8,128)S(1)} %bitcast.14, f32[2,32,32,128]{3,2,1,0:T(8,128)S(1)} %get-tuple-element.15.velocity_ref), custom_call_target="tpu_custom_call" | custom-call | flops 805306368 | bytes 2097152 | tf_op jit(solution)/shard_map/put/pallas_call | solution.py:571
  67.5 0.1 copy-done
  67.6 12.4 %sweep.1 = f32[128,512]{1,0:T(8,128)S(1)} custom-call(f32[2,128,512]{2,1,0:T(8,128)S(1)} %get-tuple-element.16.stress_ref, f32[2,128,128]{2,1,0:T(8,128)S(1)} %get-tuple-element.17.stress_edge_ref, f32[11,128,512]{2,1,0:T(8,128)S(1)} %copy-done, f32[144,256]{1,0:T(8,128)S(1)} %get-tuple-element.19.east_ref, f32[144,256]{1,0:T(8,128)S(1)} %get-tuple-element.20.west_ref, ...), custom_call_target="tpu_custom_call" | custom-call | flops 13107200 | bytes 4194304 | tf_op jit(solution)/shard_map/sweep/pallas_call | solution.py:585
  80.0 0.7 copy.16
Async XLA Ops:
  1.4 1.0 %copy-start.2 = (s32[1,32,32,128]{3,2,1,0:T(8,128)S(1)}, s32[1,32,32,128]{3,2,1,0:T(8,128)}, u32[]{:S(2)}) copy-start(s32[1,32,32,128]{3,2,1,0:T(8,128)} %param.19) | copy-start | bytes 1572868
  2.5 1.0 %copy-start.10 = (f32[2,128,512]{2,1,0:T(8,128)S(1)}, f32[2,128,512]{2,1,0:T(8,128)}, u32[]{:S(2)}) copy-start(f32[2,128,512]{2,1,0:T(8,128)} %current_hbm.1) | copy-start | bytes 1572868
  3.5 2.5 %copy-start.3 = (s32[1,32,32,128]{3,2,1,0:T(8,128)S(1)}, s32[1,32,32,128]{3,2,1,0:T(8,128)}, u32[]{:S(2)}) copy-start(s32[1,32,32,128]{3,2,1,0:T(8,128)} %param.19) | copy-start | bytes 1572868
  3.5 2.5 %copy-start.4 = (f32[1,32,32,128]{3,2,1,0:T(8,128)S(1)}, f32[1,32,32,128]{3,2,1,0:T(8,128)}, u32[]{:S(2)}) copy-start(f32[1,32,32,128]{3,2,1,0:T(8,128)} %param.20) | copy-start | bytes 1572868
  3.5 2.5 %copy-start.5 = (f32[1,32,32,128]{3,2,1,0:T(8,128)S(1)}, f32[1,32,32,128]{3,2,1,0:T(8,128)}, u32[]{:S(2)}) copy-start(f32[1,32,32,128]{3,2,1,0:T(8,128)} %param.21) | copy-start | bytes 1572868
  3.5 2.5 %copy-start.6 = (f32[128,512]{1,0:T(8,128)S(1)}, f32[128,512]{1,0:T(8,128)}, u32[]{:S(2)}) copy-start(f32[128,512]{1,0:T(8,128)} %sea_ref.1) | copy-start | bytes 786436
  3.5 2.5 %copy-start.7 = (f32[128,512]{1,0:T(8,128)S(1)}, f32[128,512]{1,0:T(8,128)}, u32[]{:S(2)}) copy-start(f32[128,512]{1,0:T(8,128)} %forcing_ref.1) | copy-start | bytes 786436
  3.5 2.5 %copy-start.8 = (f32[128,512]{1,0:T(8,128)S(1)}, f32[128,512]{1,0:T(8,128)}, u32[]{:S(2)}) copy-start(f32[128,512]{1,0:T(8,128)} %excess_ref.1) | copy-start | bytes 786436
  3.5 2.5 %copy-start.9 = (s32[128,512]{1,0:T(8,128)S(1)}, s32[128,512]{1,0:T(8,128)}, u32[]{:S(2)}) copy-start(s32[128,512]{1,0:T(8,128)} %mask_ref.1) | copy-start | bytes 786436
  5.0 1.0 %copy-start.1 = (f32[32,2,32,128]{3,2,1,0:T(8,128)}, f32[32,2,32,128]{3,2,1,0:T(8,128)S(1)}, u32[]{:S(2)}) copy-start(f32[32,2,32,128]{3,2,1,0:T(8,128)S(1)} %pick.1.values_ref) | copy-start | bytes 3145732
  65.4 2.2 %copy-start = (f32[11,128,512]{2,1,0:T(8,128)S(1)}, f32[11,128,512]{2,1,0:T(8,128)}, u32[]{:S(2)}) copy-start(f32[11,128,512]{2,1,0:T(8,128)} %get-tuple-element.18.body_ref) | copy-start | bytes 8650756
